TPU v7x, 16 devices: a whole 2x2x2 slice. The times are simulated.
16 devices in a mesh: ep: 16 (over z, y, x, core).
Axes of the slice: x: 2, y: 2, z: 2, core: 2. Of those that a mesh axis runs over, the one named last changes fastest.
Arguments:
- x: bfloat16 [16384, 1024], P('ep')
- route_idx: int32 [16384, 8], P('ep')
- gates: bfloat16 [16384, 8], P('ep')
- dy: bfloat16 [16384, 1024], P('ep')
- w1: bfloat16 [32, 1024, 512], P('ep')
- w3: bfloat16 [32, 1024, 512], P('ep')
- w2: bfloat16 [32, 512, 1024], P('ep')
Outputs:
- output 1: bfloat16 [16384, 1024], P('ep')
- output 2: bfloat16 [16384, 1024], P('ep')
- output 3: float32 [32, 1024, 512], P('ep')
- output 4: float32 [32, 1024, 512], P('ep')
- output 5: float32 [32, 512, 1024], P('ep')
All inputs are finite; a program needn't handle non-finite values.
Results may differ from a plain program's by a relative error of at most 0.00103.
Values are sent between devices in bfloat16 or wider.
A program may use at most 1 GiB of HBM per device.

v0:
```python
import jax
import jax.numpy as jnp
from jax import lax
from jax.sharding import PartitionSpec as P

HOT = 0


def _silu_parts(u):
    sig = jax.nn.sigmoid(u)
    return u * sig, sig * (1.0 + u * (1.0 - sig))


def _holders(n):
    h = n // 4 + 1
    return [(j * n) // h + j % 2 for j in range(h)]


def _slot_index(rl, nexp, cape):
    e = rl.reshape(-1)
    oh = (e[:, None] == jnp.arange(nexp)[None, :]).astype(jnp.int32)
    rank = jnp.sum((jnp.cumsum(oh, axis=0) - oh) * oh, axis=1)
    return jnp.where(e == HOT, nexp * cape, e * cape + rank)


def _exp_fwd(xr, w1, w3, w2):
    f32 = jnp.float32
    u = jnp.einsum('secd,edf->secf', xr, w1, preferred_element_type=f32)
    v = jnp.einsum('secd,edf->secf', xr, w3, preferred_element_type=f32)
    su, _ = _silu_parts(u)
    act = (su * v).astype(jnp.bfloat16)
    return jnp.einsum('secf,efd->secd', act, w2, preferred_element_type=f32).astype(jnp.bfloat16)


def _exp_bwd(xr, dr, w1, w3, w2):
    f32 = jnp.float32
    bf = jnp.bfloat16
    u = jnp.einsum('secd,edf->secf', xr, w1, preferred_element_type=f32)
    v = jnp.einsum('secd,edf->secf', xr, w3, preferred_element_type=f32)
    su, dsil = _silu_parts(u)
    act = (su * v).astype(bf)
    da = jnp.einsum('secd,efd->secf', dr, w2, preferred_element_type=f32)
    du = (da * v * dsil).astype(bf)
    dv = (da * su).astype(bf)
    dxr = (jnp.einsum('secf,edf->secd', du, w1, preferred_element_type=f32) + jnp.einsum('secf,edf->secd', dv, w3, preferred_element_type=f32)).astype(bf)
    dw1 = jnp.einsum('secd,secf->edf', xr, du, preferred_element_type=f32)
    dw3 = jnp.einsum('secd,secf->edf', xr, dv, preferred_element_type=f32)
    dw2 = jnp.einsum('secf,secd->efd', act, dr, preferred_element_type=f32)
    return dxr, dw1, dw3, dw2


def _hot_fwd(xs, w13, w2):
    f32 = jnp.float32
    u = jnp.einsum('rtd,df->rtf', xs, w13[0], preferred_element_type=f32)
    v = jnp.einsum('rtd,df->rtf', xs, w13[1], preferred_element_type=f32)
    su, _ = _silu_parts(u)
    act = (su * v).astype(jnp.bfloat16)
    return jnp.einsum('rtf,fd->rtd', act, w2, preferred_element_type=f32).astype(jnp.bfloat16)


def _hot_none_fwd(xs, w13, w2):
    return jnp.zeros_like(xs)


def _hot_bwd(xs, ds, w13, w2):
    f32 = jnp.float32
    bf = jnp.bfloat16
    u = jnp.einsum('rtd,df->rtf', xs, w13[0], preferred_element_type=f32)
    v = jnp.einsum('rtd,df->rtf', xs, w13[1], preferred_element_type=f32)
    su, dsil = _silu_parts(u)
    act = (su * v).astype(bf)
    da = jnp.einsum('rtd,fd->rtf', ds, w2, preferred_element_type=f32)
    du = (da * v * dsil).astype(bf)
    dv = (da * su).astype(bf)
    dxs = (jnp.einsum('rtf,df->rtd', du, w13[0], preferred_element_type=f32) + jnp.einsum('rtf,df->rtd', dv, w13[1], preferred_element_type=f32)).astype(bf)
    g13 = jnp.stack([jnp.einsum('rtd,rtf->df', xs, du, preferred_element_type=f32), jnp.einsum('rtd,rtf->df', xs, dv, preferred_element_type=f32)])
    g2 = jnp.einsum('rtf,rtd->fd', act, ds, preferred_element_type=f32)
    return dxs, g13, g2


def _hot_none_bwd(xs, ds, w13, w2):
    return jnp.zeros_like(xs), jnp.zeros(w13.shape, jnp.float32), jnp.zeros(w2.shape, jnp.float32)


def solution(mesh):
    n = mesh.shape['ep']
    hold = _holders(n)
    nh = len(hold)
    nwave = -(-n // nh)
    waves = [[(w * nh + j, hold[j]) for j in range(nh) if w * nh + j < n] for w in range(nwave)]
    backs = [[(b, a) for a, b in wv] for wv in waves]

    def body(xl, rl, gl, dyl, w1l, w3l, w2l):
        f32 = jnp.float32
        bf = jnp.bfloat16
        tl, d = xl.shape
        k = rl.shape[1]
        el = w1l.shape[0]
        nexp = el * n
        cape = k * (2 * tl // (nexp - 1) + 2)
        hl = HOT % el
        me = lax.axis_index('ep')
        is_holder = jnp.any(jnp.array(hold, jnp.int32) == me)
        is_owner = me == hold[0]
        idx = _slot_index(rl, nexp, cape)
        tok = jnp.arange(tl * k) // k
        g = gl.reshape(-1).astype(f32)
        gh = jnp.sum(jnp.where(rl == HOT, gl.astype(f32), 0.0), axis=1)

        hw13 = jnp.stack([w1l[hl], w3l[hl]])
        hw2 = w2l[hl]
        for j in range(1, nh):
            got13, got2 = lax.ppermute((hw13, hw2), 'ep', [(hold[0], hold[j])])
            hw13 = jnp.where(me == hold[j], got13, hw13)
            hw2 = jnp.where(me == hold[j], got2, hw2)

        send = jnp.zeros((nexp * cape, d), bf).at[idx].set(xl[tok], mode='drop')
        xr = lax.all_to_all(send, 'ep', 0, 0, tiled=True).reshape(n, el, cape, d)
        o = _exp_fwd(xr, w1l, w3l, w2l)
        back = lax.all_to_all(o.reshape(nexp * cape, d), 'ep', 0, 0, tiled=True)
        o_asg = back.at[idx].get(mode='fill', fill_value=0).astype(f32)
        ysum = (g[:, None] * o_asg).reshape(tl, k, d).sum(axis=1)

        xh = jnp.stack([lax.ppermute(xl, 'ep', wv) for wv in waves])
        ohs = lax.cond(is_holder, _hot_fwd, _hot_none_fwd, xh, hw13, hw2)
        for w in range(nwave):
            ysum = ysum + gh[:, None] * lax.ppermute(ohs[w], 'ep', backs[w]).astype(f32)
        y = ysum.astype(bf)

        do_asg = (g[:, None] * dyl[tok].astype(f32)).astype(bf)
        sendd = jnp.zeros((nexp * cape, d), bf).at[idx].set(do_asg, mode='drop')
        dr = lax.all_to_all(sendd, 'ep', 0, 0, tiled=True).reshape(n, el, cape, d)
        dxr, dw1, dw3, dw2 = _exp_bwd(xr, dr, w1l, w3l, w2l)
        backd = lax.all_to_all(dxr.reshape(nexp * cape, d), 'ep', 0, 0, tiled=True)
        dxsum = backd.at[idx].get(mode='fill', fill_value=0).astype(f32).reshape(tl, k, d).sum(axis=1)

        doh = (gh[:, None] * dyl.astype(f32)).astype(bf)
        dh = jnp.stack([lax.ppermute(doh, 'ep', wv) for wv in waves])
        dxs, g13, g2 = lax.cond(is_holder, _hot_bwd, _hot_none_bwd, xh, dh, hw13, hw2)
        for w in range(nwave):
            dxsum = dxsum + lax.ppermute(dxs[w], 'ep', backs[w]).astype(f32)
        dx = dxsum.astype(bf)

        acc13 = g13
        acc2 = g2
        for j in range(1, nh):
            got13, got2 = lax.ppermute((g13, g2), 'ep', [(hold[j], hold[0])])
            acc13 = acc13 + got13
            acc2 = acc2 + got2
        dw1 = dw1.at[hl].add(jnp.where(is_owner, acc13[0], 0.0))
        dw3 = dw3.at[hl].add(jnp.where(is_owner, acc13[1], 0.0))
        dw2 = dw2.at[hl].add(jnp.where(is_owner, acc2, 0.0))
        return y, dx, dw1, dw3, dw2

    spec_t = P('ep', None)
    spec_w = P('ep', None, None)
    return jax.shard_map(body, mesh=mesh, in_specs=(spec_t, spec_t, spec_t, spec_t, spec_w, spec_w, spec_w), out_specs=(spec_t, spec_t, spec_w, spec_w, spec_w), check_vma=False)
```

profile of v0, /device:TPU:0, one launch (start us, length us, event | category | flops | bytes accessed | tf_op | source)
XLA Modules:
  0.0 2976.1 jit_solution(11738252203252141244)
XLA Ops:
  42.8 37.9 %gather_fusion.2 = bf16[8192,1024]{1,0:T(8,128)(2,1)} fusion(bf16[1024,1024]{1,0:T(8,128)(2,1)S(1)} %copy-done, s32[8192]{0:T(1024)} %broadcast_clamp_fusion.2), kind=kCustom, calls=%fused_computation.2 | custom fusion | bytes 33587200 | tf_op jit(solution)/shard_map/gather | solution.py:130
  95.4 141.9 %scatter_custom_fusion.1 = bf16[17408,1024]{1,0:T(8,128)(2,1)} fusion(s32[8192]{0:T(1024)S(1)} %get-tuple-element.72, bf16[]{:T(256)} %constant.122.clone.1, bf16[8192,1024]{1,0:T(8,128)(2,1)} %multiply_convert_fusion.8, s32[8192]{0:T(1024)S(1)} %broadcast_clamp_fusion.1), kind=kCustom, calls=%fused_computation.77 | custom fusion | bytes 35652096 | tf_op jit(solution)/shard_map/scatter | solution.py:131
  242.6 35.6 %gather_fusion = bf16[8192,1024]{1,0:T(8,128)(2,1)} fusion(bf16[1024,1024]{1,0:T(8,128)(2,1)S(1)} %copy-done.2, s32[8192]{0:T(1024)S(1)} %copy-done.25), kind=kCustom, calls=%fused_computation | custom fusion | bytes 33587200 | tf_op jit(solution)/shard_map/gather | solution.py:117
  278.2 132.3 %scatter_custom_fusion = bf16[17408,1024]{1,0:T(8,128)(2,1)} fusion(s32[8192]{0:T(1024)S(1)} %get-tuple-element.72, bf16[]{:T(256)} %constant.122.clone.1, bf16[8192,1024]{1,0:T(8,128)(2,1)} %gather_fusion, s32[8192]{0:T(1024)S(1)} %broadcast_clamp_fusion.1), kind=kCustom, calls=%fused_computation.79 | custom fusion | bytes 35652096 | tf_op jit(solution)/shard_map/scatter | solution.py:117
  410.5 261.7 %all-to-all-done.2 = bf16[16,1088,1024]{2,1,0:T(8,128)(2,1)} async-done(((bf16[16,1088,1024]{2,1,0:T(8,128)(2,1)}), bf16[16,1088,1024]{2,1,0:T(8,128)(2,1)}, u32[]{:S(2)}, u32[]{:S(2)}) %all-to-all-start.2) | async-done | bytes 35651616 | tf_op jit(solution)/shard_map/all_to_all | solution.py:132
  677.5 30.6 %fusion.44 = f32[2,16,544,512]{3,2,1,0:T(8,128)} fusion(bf16[16,2,544,1024]{3,2,1,0:T(8,128)(2,1)} %bitcast.45, bf16[2,512,1024]{2,1,0:T(8,128)(2,1)S(1)} %copy-done.18), kind=kOutput, calls=%fused_computation.67 | convolution fusion | flops 18253611008 | bytes 73400320 | tf_op jit(solution)/shard_map/secd,efd->secf/dot_general | solution.py:42
  708.2 395.1 %all-to-all-done = bf16[16,1088,1024]{2,1,0:T(8,128)(2,1)} async-done(((bf16[16,1088,1024]{2,1,0:T(8,128)(2,1)}), bf16[16,1088,1024]{2,1,0:T(8,128)(2,1)}, u32[]{:S(2)}, u32[]{:S(2)}) %all-to-all-start) | async-done | bytes 35651616 | tf_op jit(solution)/shard_map/all_to_all | solution.py:118
  1103.2 31.0 %fusion.48 = f32[2,16,544,512]{3,2,1,0:T(8,128)} fusion(bf16[16,2,544,1024]{3,2,1,0:T(8,128)(2,1)} %bitcast.22, bf16[2,1024,512]{2,1,0:T(8,128)(2,1)} %param.22), kind=kOutput, calls=%fused_computation.71 | convolution fusion | flops 18253611008 | bytes 73400320 | tf_op jit(solution)/shard_map/secd,edf->secf/dot_general | solution.py:28
  1134.2 61.6 %fusion.36 = (bf16[16,2,544,512]{3,2,0,1:T(8,128)(2,1)}, bf16[16,2,544,512]{3,2,0,1:T(8,128)(2,1)}, bf16[16,2,544,512]{3,2,0,1:T(8,128)(2,1)}) fusion(f32[2,16,544,512]{3,2,1,0:T(8,128)} %fusion.48, f32[2,16,544,512]{3,2,1,0:T(8,128)} %fusion.44, bf16[2,1024,512]{2,1,0:T(8,128)(2,1)} %param.23, bf16[16,2,544,1024]{3,2,1,0:T(8,128)(2,1)} %bitcast.22), kind=kOutput, calls=%fused_computation.52 | convolution fusion | flops 18387304448 | bytes 162529280 | tf_op jit(solution)/shard_map/secd,edf->secf/dot_general | solution.py:29
  1195.9 30.5 %convert_bitcast_fusion = bf16[16,2,544,1024]{3,2,0,1:T(8,128)(2,1)} fusion(bf16[16,2,544,512]{3,2,0,1:T(8,128)(2,1)} %get-tuple-element.82, bf16[2,512,1024]{2,1,0:T(8,128)(2,1)S(1)} %copy-done.19), kind=kOutput, calls=%fused_computation.61 | convolution fusion | flops 18271436800 | bytes 55574528 | tf_op jit(solution)/shard_map/secf,efd->secd/dot_general | solution.py:32
  1255.6 34.6 %fusion.80 = f32[2,16,544,1024]{3,2,1,0:T(8,128)} fusion(bf16[16,2,544,512]{3,2,0,1:T(8,128)(2,1)} %get-tuple-element.83, bf16[2,1024,512]{2,1,0:T(8,128)(2,1)S(1)} %copy-done.24), kind=kOutput, calls=%fused_computation.109 | convolution fusion | flops 18253611008 | bytes 91226112 | tf_op jit(solution)/shard_map/secf,edf->secd/dot_general | solution.py:45
  1290.2 41.9 %fusion.32 = bf16[16,2,544,1024]{3,2,0,1:T(8,128)(2,1)} fusion(f32[2,16,544,1024]{3,2,1,0:T(8,128)} %fusion.80, bf16[16,2,544,512]{3,2,0,1:T(8,128)(2,1)} %get-tuple-element.84, bf16[2,1024,512]{2,1,0:T(8,128)(2,1)} %param.23), kind=kOutput, calls=%fused_computation.45 | convolution fusion | flops 18289262592 | bytes 126877696 | tf_op jit(solution)/shard_map/secf,edf->secd/dot_general | solution.py:45
  1356.3 325.0 %all-to-all-done.1 = bf16[16,1088,1024]{2,1,0:T(8,128)(2,1)} async-done(((bf16[16,1088,1024]{2,1,0:T(8,128)(2,1)}), bf16[16,1088,1024]{2,1,0:T(8,128)(2,1)}, u32[]{:S(2)}, u32[]{:S(2)}) %all-to-all-start.1) | async-done | bytes 35651616 | tf_op jit(solution)/shard_map/all_to_all | solution.py:120
  1694.1 352.7 %collective-permute-done = bf16[2,1024,512]{2,1,0:T(8,128)(2,1)} collective-permute-done((bf16[2,1024,512]{2,1,0:T(8,128)(2,1)}, bf16[2,1024,512]{2,1,0:T(8,128)(2,1)}, u32[]{:S(2)}, u32[]{:S(2)}) %collective-permute-start) | collective-permute-done | bytes 2097184 | tf_op jit(solution)/shard_map/ppermute | solution.py:113
  2059.8 74.4 %collective-permute-done.1 = bf16[2,1024,512]{2,1,0:T(8,128)(2,1)} collective-permute-done((bf16[2,1024,512]{2,1,0:T(8,128)(2,1)}, bf16[2,1024,512]{2,1,0:T(8,128)(2,1)}, u32[]{:S(2)}, u32[]{:S(2)}) %collective-permute-start.1) | collective-permute-done | bytes 2097184 | tf_op jit(solution)/shard_map/ppermute | solution.py:113
  2289.4 150.6 %gather_fusion.1 = bf16[8192,1024]{1,0:T(8,128)(2,1)} fusion(bf16[17408,1024]{1,0:T(8,128)(2,1)} %bitcast.33, s32[8192]{0:T(1024)S(1)} %broadcast_clamp_fusion), kind=kCustom, calls=%fused_computation.1 | custom fusion | bytes 33587200 | tf_op jit(solution)/shard_map/gather | solution.py:121
  2440.0 150.9 %gather_fusion.3 = bf16[8192,1024]{1,0:T(8,128)(2,1)} fusion(bf16[17408,1024]{1,0:T(8,128)(2,1)} %bitcast.52, s32[8192]{0:T(1024)S(1)} %broadcast_clamp_fusion), kind=kCustom, calls=%fused_computation.3 | custom fusion | bytes 33587200 | tf_op jit(solution)/shard_map/gather | solution.py:121
  2591.0 26.9 convert_reduce_fusion
  2645.8 30.5 %collective-permute-done.19 = bf16[1024,1024]{1,0:T(8,128)(2,1)} collective-permute-done((bf16[1024,1024]{1,0:T(8,128)(2,1)}, bf16[1024,1024]{1,0:T(8,128)(2,1)}, u32[]{:S(2)}, u32[]{:S(2)}) %collective-permute-start.19) | collective-permute-done | bytes 2097184 | tf_op jit(solution)/shard_map/ppermute | solution.py:138
  2681.4 89.0 %conditional.3 = (bf16[4,1024,1024]{2,1,0:T(8,128)(2,1)}, f32[512,1024]{1,0:T(8,128)}, f32[2,1024,512]{2,1,0:T(8,128)}) conditional(s32[]{:T(128)} %convert_element_type.122, () %tuple.36, (bf16[4,1024,1024]{2,1,0:T(8,128)(2,1)S(1)}, bf16[512,1024]{1,0:T(8,128)(2,1)}, bf16[2,1024,512]{2,1,0:T(8,128)(2,1)S(1)}, ...), branch_computations={%region_11.12_spmd, %region_12.13_spmd} | conditional | flops 34409021440 | bytes 305135808 | solution.py:139
  2779.1 27.4 fusion.70
  2821.1 27.6 fusion.64
  2870.0 27.6 fusion.67
  2912.0 29.1 collective-permute-done.27
  (190 shorter events, 542.0 us)
Async XLA Ops:
  237.3 434.9 %all-to-all-start.2 = ((bf16[16,1088,1024]{2,1,0:T(8,128)(2,1)}), bf16[16,1088,1024]{2,1,0:T(8,128)(2,1)}, u32[]{:S(2)}, u32[]{:S(2)}) async-start(bf16[16,1088,1024]{2,1,0:T(8,128)(2,1)} %bitcast.204), calls=%async_computation.2 | async-start | bytes 71303168 | tf_op jit(solution)/shard_map/all_to_all | solution.py:132
  672.2 431.0 %all-to-all-start = ((bf16[16,1088,1024]{2,1,0:T(8,128)(2,1)}), bf16[16,1088,1024]{2,1,0:T(8,128)(2,1)}, u32[]{:S(2)}, u32[]{:S(2)}) async-start(bf16[16,1088,1024]{2,1,0:T(8,128)(2,1)} %bitcast.203), calls=%async_computation | async-start | bytes 71303168 | tf_op jit(solution)/shard_map/all_to_all | solution.py:118
  1250.4 430.8 %all-to-all-start.1 = ((bf16[16,1088,1024]{2,1,0:T(8,128)(2,1)}), bf16[16,1088,1024]{2,1,0:T(8,128)(2,1)}, u32[]{:S(2)}, u32[]{:S(2)}) async-start(bf16[16,1088,1024]{2,1,0:T(8,128)(2,1)} %bitcast.205), calls=%async_computation.1 | async-start | bytes 71303168 | tf_op jit(solution)/shard_map/all_to_all | solution.py:120
  1681.2 758.8 %all-to-all-start.3 = ((bf16[16,1088,1024]{2,1,0:T(8,128)(2,1)}), bf16[16,1088,1024]{2,1,0:T(8,128)(2,1)}, u32[]{:S(2)}, u32[]{:S(2)}) async-start(bf16[16,1088,1024]{2,1,0:T(8,128)(2,1)} %bitcast.202), calls=%async_computation.3 | async-start | bytes 71303168 | tf_op jit(solution)/shard_map/all_to_all | solution.py:134
  1689.1 357.7 %collective-permute-start = (bf16[2,1024,512]{2,1,0:T(8,128)(2,1)}, bf16[2,1024,512]{2,1,0:T(8,128)(2,1)}, u32[]{:S(2)}, u32[]{:S(2)}) collective-permute-start(bf16[2,1024,512]{2,1,0:T(8,128)(2,1)} %pad_maximum_fusion.3), channel_id=1, source_target_pairs={{0,4}} | collective-permute-start | bytes 6291464 | tf_op jit(solution)/shard_map/ppermute | solution.py:113
  2048.4 85.8 %collective-permute-start.1 = (bf16[2,1024,512]{2,1,0:T(8,128)(2,1)}, bf16[2,1024,512]{2,1,0:T(8,128)(2,1)}, u32[]{:S(2)}, u32[]{:S(2)}) collective-permute-start(bf16[2,1024,512]{2,1,0:T(8,128)(2,1)} %broadcast_select_fusion), channel_id=1, source_target_pairs={{0,6}} | collective-permute-start | bytes 6291464 | tf_op jit(solution)/shard_map/ppermute | solution.py:113
  2053.4 83.9 %collective-permute-start.8 = (bf16[512,1024]{1,0:T(8,128)(2,1)}, bf16[512,1024]{1,0:T(8,128)(2,1)}, u32[]{:S(2)}, u32[]{:S(2)}) collective-permute-start(bf16[512,1024]{1,0:T(8,128)(2,1)} %slice_bitcast_fusion.8), channel_id=1, source_target_pairs={{0,4}} | collective-permute-start | bytes 3145736 | tf_op jit(solution)/shard_map/ppermute | solution.py:113
  2142.9 56.1 %collective-permute-start.5 = (bf16[1024,1024]{1,0:T(8,128)(2,1)S(1)}, bf16[1024,1024]{1,0:T(8,128)(2,1)}, u32[]{:S(2)}, u32[]{:S(2)}) collective-permute-start(bf16[1024,1024]{1,0:T(8,128)(2,1)S(1)} %copy-done.3), channel_id=1, source_target_pairs={{5,0},{6,4},{7,6},{8,10},{9,12}} | collective-permute-start | bytes 6291464 | tf_op jit(solution)/shard_map/ppermute | solution.py:124
  2144.2 56.2 %collective-permute-start.4 = (bf16[1024,1024]{1,0:T(8,128)(2,1)S(1)}, bf16[1024,1024]{1,0:T(8,128)(2,1)}, u32[]{:S(2)}, u32[]{:S(2)}) collective-permute-start(bf16[1024,1024]{1,0:T(8,128)(2,1)S(1)} %copy-done.3), channel_id=1, source_target_pairs={{0,0},{1,4},{2,6},{3,10},{4,12}} | collective-permute-start | bytes 6291464 | tf_op jit(solution)/shard_map/ppermute | solution.py:124
  2146.2 54.2 %collective-permute-start.7 = (bf16[1024,1024]{1,0:T(8,128)(2,1)S(1)}, bf16[1024,1024]{1,0:T(8,128)(2,1)}, u32[]{:S(2)}, u32[]{:S(2)}) collective-permute-start(bf16[1024,1024]{1,0:T(8,128)(2,1)S(1)} %copy-done.3), channel_id=1, source_target_pairs={{15,0}} | collective-permute-start | bytes 6291464 | tf_op jit(solution)/shard_map/ppermute | solution.py:124
  2264.4 353.5 %collective-permute-start.12 = (bf16[1024,1024]{1,0:T(8,128)(2,1)}, bf16[1024,1024]{1,0:T(8,128)(2,1)}, u32[]{:S(2)}, u32[]{:S(2)}) collective-permute-start(bf16[1024,1024]{1,0:T(8,128)(2,1)} %get-tuple-element.89), channel_id=1, source_target_pairs={{0,0},{4,1},{6,2},{10,3},{12,4}} | collective-permute-start | bytes 6291464 | tf_op jit(solution)/shard_map/ppermute | solution.py:127
  2281.6 336.3 %collective-permute-start.15 = (bf16[1024,1024]{1,0:T(8,128)(2,1)}, bf16[1024,1024]{1,0:T(8,128)(2,1)}, u32[]{:S(2)}, u32[]{:S(2)}) collective-permute-start(bf16[1024,1024]{1,0:T(8,128)(2,1)} %get-tuple-element.90), channel_id=1, source_target_pairs={{0,15}} | collective-permute-start | bytes 6291464 | tf_op jit(solution)/shard_map/ppermute | solution.py:127
  2284.2 333.7 %collective-permute-start.14 = (bf16[1024,1024]{1,0:T(8,128)(2,1)}, bf16[1024,1024]{1,0:T(8,128)(2,1)}, u32[]{:S(2)}, u32[]{:S(2)}) collective-permute-start(bf16[1024,1024]{1,0:T(8,128)(2,1)} %get-tuple-element.91), channel_id=1, source_target_pairs={{0,10},{4,11},{6,12},{10,13},{12,14}} | collective-permute-start | bytes 6291464 | tf_op jit(solution)/shard_map/ppermute | solution.py:127
  2286.8 331.1 %collective-permute-start.13 = (bf16[1024,1024]{1,0:T(8,128)(2,1)}, bf16[1024,1024]{1,0:T(8,128)(2,1)}, u32[]{:S(2)}, u32[]{:S(2)}) collective-permute-start(bf16[1024,1024]{1,0:T(8,128)(2,1)} %get-tuple-element.92), channel_id=1, source_target_pairs={{0,5},{4,6},{6,7},{10,8},{12,9}} | collective-permute-start | bytes 6291464 | tf_op jit(solution)/shard_map/ppermute | solution.py:127
  2624.7 51.6 %collective-permute-start.19 = (bf16[1024,1024]{1,0:T(8,128)(2,1)}, bf16[1024,1024]{1,0:T(8,128)(2,1)}, u32[]{:S(2)}, u32[]{:S(2)}) collective-permute-start(bf16[1024,1024]{1,0:T(8,128)(2,1)} %get-tuple-element.95), channel_id=1, source_target_pairs={{15,0}} | collective-permute-start | bytes 6291464 | tf_op jit(solution)/shard_map/ppermute | solution.py:138
  2626.0 51.0 %collective-permute-start.18 = (bf16[1024,1024]{1,0:T(8,128)(2,1)}, bf16[1024,1024]{1,0:T(8,128)(2,1)}, u32[]{:S(2)}, u32[]{:S(2)}) collective-permute-start(bf16[1024,1024]{1,0:T(8,128)(2,1)} %get-tuple-element.95), channel_id=1, source_target_pairs={{10,0},{11,4},{12,6},{13,10},{14,12}} | collective-permute-start | bytes 6291464 | tf_op jit(solution)/shard_map/ppermute | solution.py:138
  2806.4 56.8 %collective-permute-start.31 = (f32[512,1024]{1,0:T(8,128)}, f32[512,1024]{1,0:T(8,128)}, u32[]{:S(2)}, u32[]{:S(2)}) collective-permute-start(f32[512,1024]{1,0:T(8,128)} %get-tuple-element.70), channel_id=1, source_target_pairs={{12,0}} | collective-permute-start | bytes 6291464 | tf_op jit(solution)/shard_map/ppermute | solution.py:147
  2807.7 56.8 %collective-permute-start.30 = (f32[512,1024]{1,0:T(8,128)}, f32[512,1024]{1,0:T(8,128)}, u32[]{:S(2)}, u32[]{:S(2)}) collective-permute-start(f32[512,1024]{1,0:T(8,128)} %get-tuple-element.70), channel_id=1, source_target_pairs={{10,0}} | collective-permute-start | bytes 6291464 | tf_op jit(solution)/shard_map/ppermute | solution.py:147
  2809.0 56.8 %collective-permute-start.29 = (f32[512,1024]{1,0:T(8,128)}, f32[512,1024]{1,0:T(8,128)}, u32[]{:S(2)}, u32[]{:S(2)}) collective-permute-start(f32[512,1024]{1,0:T(8,128)} %get-tuple-element.70), channel_id=1, source_target_pairs={{6,0}} | collective-permute-start | bytes 6291464 | tf_op jit(solution)/shard_map/ppermute | solution.py:147
  2810.3 56.8 %collective-permute-start.28 = (f32[512,1024]{1,0:T(8,128)}, f32[512,1024]{1,0:T(8,128)}, u32[]{:S(2)}, u32[]{:S(2)}) collective-permute-start(f32[512,1024]{1,0:T(8,128)} %get-tuple-element.70), channel_id=1, source_target_pairs={{4,0}} | collective-permute-start | bytes 6291464 | tf_op jit(solution)/shard_map/ppermute | solution.py:147
  2861.9 79.1 %collective-permute-start.27 = (f32[2,1024,512]{2,1,0:T(8,128)}, f32[2,1024,512]{2,1,0:T(8,128)}, u32[]{:S(2)}, u32[]{:S(2)}) collective-permute-start(f32[2,1024,512]{2,1,0:T(8,128)} %get-tuple-element.71), channel_id=1, source_target_pairs={{12,0}} | collective-permute-start | bytes 12582920 | tf_op jit(solution)/shard_map/ppermute | solution.py:147
  2863.2 94.8 %collective-permute-start.26 = (f32[2,1024,512]{2,1,0:T(8,128)}, f32[2,1024,512]{2,1,0:T(8,128)}, u32[]{:S(2)}, u32[]{:S(2)}) collective-permute-start(f32[2,1024,512]{2,1,0:T(8,128)} %get-tuple-element.71), channel_id=1, source_target_pairs={{10,0}} | collective-permute-start | bytes 12582920 | tf_op jit(solution)/shard_map/ppermute | solution.py:147
  2864.5 93.5 %collective-permute-start.25 = (f32[2,1024,512]{2,1,0:T(8,128)}, f32[2,1024,512]{2,1,0:T(8,128)}, u32[]{:S(2)}, u32[]{:S(2)}) collective-permute-start(f32[2,1024,512]{2,1,0:T(8,128)} %get-tuple-element.71), channel_id=1, source_target_pairs={{6,0}} | collective-permute-start | bytes 12582920 | tf_op jit(solution)/shard_map/ppermute | solution.py:147
  2865.8 94.9 %collective-permute-start.24 = (f32[2,1024,512]{2,1,0:T(8,128)}, f32[2,1024,512]{2,1,0:T(8,128)}, u32[]{:S(2)}, u32[]{:S(2)}) collective-permute-start(f32[2,1024,512]{2,1,0:T(8,128)} %get-tuple-element.71), channel_id=1, source_target_pairs={{4,0}} | collective-permute-start | bytes 12582920 | tf_op jit(solution)/shard_map/ppermute | solution.py:147
  (43 other events, 2096.1 us)
where the time goes:
time: 3020 us; the launch traced here: 2980 us
  waiting for transfers between devices  1550 us (51%)
  local copies, waits for them, and re-layouts  730 us (24%)
  matrix products  418 us (14%)
  other arithmetic  142 us (5%)
  starting transfers between devices  130 us (4%)
    ppermute x8, waiting for transfers between devices, body(): got13, got2 = lax.ppermute((hw13, hw2), 'ep', [(hold[0], hold[j])])  478 us
    all_to_all x1, waiting for transfers between devices, body(): xr = lax.all_to_all(send, 'ep', 0, 0, tiled=True).reshape(n, el, cape, d)  395 us
    all_to_all x1, waiting for transfers between devices, body(): back = lax.all_to_all(o.reshape(nexp * cape, d), 'ep', 0, 0, tiled=True)  325 us
    gather x2, local copies, waits for them, and re-layouts, body(): o_asg = back.at[idx].get(mode='fill', fill_value=0).astype(f32)  302 us
    all_to_all x1, waiting for transfers between devices, body(): dr = lax.all_to_all(sendd, 'ep', 0, 0, tiled=True).reshape(n, el, cape, d)  262 us
    scatter x1, local copies, waits for them, and re-layouts, body(): sendd = jnp.zeros((nexp * cape, d), bf).at[idx].set(do_asg, mode='drop')  142 us
    scatter x2, local copies, waits for them, and re-layouts, body(): send = jnp.zeros((nexp * cape, d), bf).at[idx].set(xl[tok], mode='drop')  132 us
    dot_general x1, matrix products, _exp_fwd(): v = jnp.einsum('secd,edf->secf', xr, w3, preferred_element_type=f32)  61.6 us
  transfers between devices with their start and end apart: 36, of which 15 were waited for; matrix products, arithmetic and copies ran while one was open for 26% of the time, Pallas kernels for 0%

commit v1 on v0

v1 whole, which is shorter than its diff:
```python
import functools

import jax
import jax.numpy as jnp
from jax import lax
from jax.experimental import pallas as pl
from jax.experimental.pallas import tpu as pltpu
from jax.sharding import PartitionSpec as P

F32 = jnp.float32
BF = jnp.bfloat16
SUB = 256
CHUNKS = 4
NT = (((1,), (1,)), ((), ()))
TN = (((0,), (0,)), ((), ()))


def _dot(a, b):
    return jnp.dot(a, b, preferred_element_type=F32)


def _dot_nt(a, b):
    return lax.dot_general(a, b, NT, preferred_element_type=F32)


def _dot_tn(a, b):
    return lax.dot_general(a, b, TN, preferred_element_type=F32)


def _inner(x, dy, g, w1, w3, w2):
    on = g > 0.0
    u = _dot(x, w1)
    v = _dot(x, w3)
    sig = jax.nn.sigmoid(u)
    su = u * sig
    do = (g * dy.astype(F32)).astype(BF)
    da = _dot_nt(do, w2)
    act = jnp.where(on, su * v, 0.0).astype(BF)
    du = jnp.where(on, da * v * (sig * (1.0 + u * (1.0 - sig))), 0.0).astype(BF)
    dv = jnp.where(on, da * su, 0.0).astype(BF)
    return act, do, du, dv


def _home_kernel(slot, el, gd_ref, x_ref, dy_ref, w1_ref, w3_ref, w2_ref, yin_ref, dxin_ref, y_ref, dx_ref):
    s = pl.program_id(0)
    e = s * el + slot

    @pl.when(s == 0)
    def _():
        y_ref[...] = yin_ref[...]
        dx_ref[...] = dxin_ref[...]

    tl = x_ref.shape[0]
    w1 = w1_ref[0]
    w3 = w3_ref[0]
    w2 = w2_ref[0]

    @pl.loop(0, tl // SUB)
    def _(i):
        r = pl.ds(pl.multiple_of(i * SUB, SUB), SUB)
        gd = gd_ref[r, :]
        lane = lax.broadcasted_iota(jnp.int32, gd.shape, 1)
        g = jnp.sum(jnp.where(lane == e, gd, 0.0), axis=1, keepdims=True)
        act, _, du, dv = _inner(x_ref[r, :], dy_ref[r, :], g, w1, w3, w2)
        on = g > 0.0
        o = _dot(act, w2).astype(BF).astype(F32)
        y_ref[r, :] += jnp.where(on, g * o, 0.0)
        dxk = (_dot_nt(du, w1) + _dot_nt(dv, w3)).astype(BF).astype(F32)
        dx_ref[r, :] += jnp.where(on, dxk, 0.0)


def _home(slot, el, gd, x, dy, w1, w3, w2, y, dx):
    n, d, ff = w1.shape
    tl = x.shape[0]
    full = lambda a: pl.BlockSpec(a.shape, lambda s: (0,) * a.ndim, pipeline_mode=pl.Buffered(1))
    per = lambda a: pl.BlockSpec((1,) + a.shape[1:], lambda s: (s, 0, 0))
    return pl.pallas_call(
        functools.partial(_home_kernel, slot, el),
        grid=(n,),
        in_specs=[full(gd), full(x), full(dy), per(w1), per(w3), per(w2), full(y), full(dx)],
        out_specs=[full(y), full(dx)],
        out_shape=[jax.ShapeDtypeStruct(y.shape, F32)] * 2,
        input_output_aliases={6: 0, 7: 1},
        compiler_params=pltpu.CompilerParams(vmem_limit_bytes=60 << 20),
        cost_estimate=pl.CostEstimate(flops=n * tl * d * ff * 12, bytes_accessed=n * d * ff * 6, transcendentals=0),
        name='home',
    )(gd, x, dy, w1, w3, w2, y, dx)


def _owner_kernel(el, g_ref, x_ref, dy_ref, w1_ref, w3_ref, w2_ref, i1_ref, i3_ref, i2_ref, d1_ref, d3_ref, d2_ref):
    @pl.when(pl.program_id(0) == 0)
    def _():
        d1_ref[...] = i1_ref[...]
        d3_ref[...] = i3_ref[...]
        d2_ref[...] = i2_ref[...]

    x = x_ref[...]
    dy = dy_ref[...]
    gd = g_ref[...]

    @pl.loop(0, el)
    def _(e):
        lane = lax.broadcasted_iota(jnp.int32, gd.shape, 1)
        g = jnp.sum(jnp.where(lane == e, gd, 0.0), axis=1, keepdims=True)
        act, do, du, dv = _inner(x, dy, g, w1_ref[e], w3_ref[e], w2_ref[e])
        d1_ref[e] += _dot_tn(x, du)
        d3_ref[e] += _dot_tn(x, dv)
        d2_ref[e] += _dot_tn(act, do)


def _owner(gt, x, dy, w1, w3, w2, a1, a3, a2, block):
    el, d, ff = w1.shape
    rows = x.shape[0]
    full = lambda a: pl.BlockSpec(a.shape, lambda s: (0,) * a.ndim, pipeline_mode=pl.Buffered(1))
    per = lambda a: pl.BlockSpec((block, a.shape[1]), lambda s: (s, 0))
    return pl.pallas_call(
        functools.partial(_owner_kernel, el),
        grid=(rows // block,),
        in_specs=[per(gt), per(x), per(dy)] + [full(a) for a in (w1, w3, w2, a1, a3, a2)],
        out_specs=[full(a) for a in (a1, a3, a2)],
        out_shape=[jax.ShapeDtypeStruct(a.shape, F32) for a in (a1, a3, a2)],
        input_output_aliases={6: 0, 7: 1, 8: 2},
        compiler_params=pltpu.CompilerParams(vmem_limit_bytes=60 << 20),
        cost_estimate=pl.CostEstimate(flops=rows * el * d * ff * 12, bytes_accessed=rows * d * 4, transcendentals=0),
        name='owner',
    )(gt, x, dy, w1, w3, w2, a1, a3, a2)


def solution(mesh):
    n = mesh.shape['ep']

    def body(xl, rl, gl, dyl, w1l, w3l, w2l):
        tl, d = xl.shape
        el, _, ff = w1l.shape
        nexp = el * n
        gather = lambda a: lax.all_gather(a, 'ep', axis=0, tiled=True)
        hit = rl[:, :, None] == jnp.arange(nexp)[None, None, :]
        gd = jnp.sum(jnp.where(hit, gl.astype(F32)[:, :, None], 0.0), axis=1)
        mine = lax.all_to_all(gd.reshape(tl, n, el).transpose(1, 0, 2), 'ep', 0, 0, tiled=True)

        ws = [[gather(a[s:s + 1]) for a in (w1l, w3l, w2l)] for s in range(el)]
        ws[0][0], xg, dyg = lax.optimization_barrier((ws[0][0], xl, dyl))
        y = jnp.zeros((tl, d), F32)
        dx = jnp.zeros((tl, d), F32)
        for s in range(el):
            y, dx = _home(s, el, gd, xl, dyl, *ws[s], y, dx)

        step = tl // CHUNKS
        acc = (jnp.zeros((el, d, ff), F32), jnp.zeros((el, d, ff), F32), jnp.zeros((el, ff, d), F32))
        for c in range(CHUNKS):
            r = slice(c * step, (c + 1) * step)
            gt = mine[:, r].reshape(n * step, el)
            acc = _owner(gt, gather(xg[r]), gather(dyg[r]), w1l, w3l, w2l, *acc, 512)
        return (y.astype(BF), dx.astype(BF)) + tuple(acc)

    spec_t = P('ep', None)
    spec_w = P('ep', None, None)
    return jax.shard_map(body, mesh=mesh, in_specs=(spec_t, spec_t, spec_t, spec_t, spec_w, spec_w, spec_w), out_specs=(spec_t, spec_t, spec_w, spec_w, spec_w), check_vma=False)
```

time: 3020 us -> 972 us (0.32); the launches traced: 2980 us -> 972 us
  waiting for transfers between devices: 1550 us -> 349 us
  local copies, waits for them, and re-layouts: 730 us -> 34.5 us
  Pallas kernels: 0 us -> 566 us
  matrix products: 418 us -> 0 us
  other arithmetic: 142 us -> 5.75 us
  starting transfers between devices: 130 us -> 3.02 us
    all_to_all x4 -> x1, waiting for transfers between devices: 982 us -> 6.83 us  [body(): lax.all_to_all(gd.reshape(tl, n, el).transpose(1, 0, 2), 'ep', 0, 0, tile...]
    ppermute x32 -> x0, waiting for transfers between devices: 572 us -> none  [the longest x8 478 us: body(): got13, got2 = lax.ppermute((hw13, hw2), 'ep', [(hold[0], hold[j])])]
    pallas_call x0 -> x6, Pallas kernels: none -> 566 us  [the longest x4 294 us: _owner(): pl.pallas_call(functools.partial(_owner_kernel, el), grid=(rows // block,...]
    dot_general x19 -> x0, matrix products: 418 us -> none  [the longest x1 61.6 us: _exp_fwd(): v = jnp.einsum('secd,edf->secf', xr, w3, preferred_element_type=f32)]
    gather x4 -> x0, local copies, waits for them, and re-layouts: 375 us -> none  [the longest x2 302 us: body(): o_asg = back.at[idx].get(mode='fill', fill_value=0).astype(f32)]
    all_gather x0 -> x14, waiting for transfers between devices: none -> 337 us  [body(): gather = lambda a: lax.all_gather(a, 'ep', axis=0, tiled=True)]
    scatter x3 -> x0, local copies, waits for them, and re-layouts: 274 us -> none  [the longest x1 142 us: body(): sendd = jnp.zeros((nexp * cape, d), bf).at[idx].set(do_asg, mode='drop')]
    ppermute x32 -> x0, starting transfers between devices: 110 us -> none  [the longest x8 31.5 us: body(): got13, got2 = lax.ppermute((hw13, hw2), 'ep', [(hold[0], hold[j])])]
  transfers between devices with their start and end apart: 36 -> 15, of which waited for: 15 -> 8; matrix products, arithmetic and copies ran while one was open for 26% -> 4% of each run, Pallas kernels for 0% -> 51%
where the time goes in v1:
time: 972 us
  Pallas kernels  566 us (58%)
  waiting for transfers between devices  349 us (36%)
  local copies, waits for them, and re-layouts  34.5 us (4%)
  between operations  14 us (1%)
    all_gather x14, waiting for transfers between devices, body(): gather = lambda a: lax.all_gather(a, 'ep', axis=0, tiled=True)  337 us
    pallas_call x4, Pallas kernels, _owner(): pl.pallas_call(functools.partial(_owner_kernel, el), grid=(rows // block,...  294 us
    pallas_call x2, Pallas kernels, _home(): pl.pallas_call(functools.partial(_home_kernel, slot, el), grid=(n,), in_s...  272 us
  transfers between devices with their start and end apart: 15, of which 8 were waited for; matrix products, arithmetic and copies ran while one was open for 4% of the time, Pallas kernels for 51%

profile of v1, /device:TPU:0, one launch (start us, length us, event | category | flops | bytes accessed | tf_op | source)
XLA Modules:
  0.0 971.7 jit_solution(3595826054711961990)
XLA Ops:
  7.2 3.1 fusion.4
  12.0 3.2 fusion.2
  17.0 72.7 %all-gather.21.cloned.1.call-done.w1_ref = bf16[16,1024,512]{2,1,0:T(8,128)(2,1)} async-done(((bf16[1,1024,512]{2,1,0:T(8,128)(2,1)}), bf16[16,1024,512]{2,1,0:T(8,128)(2,1)}) %all-gather.21.cloned.1.call-update) | async-done | bytes 16777232 | tf_op jit(solution)/shard_map/all_gather | solution.py:136
  91.2 2.9 fusion
  98.3 2.5 all-to-all-start
  101.8 6.8 all-to-all-done
  116.7 53.3 %all-gather.23.cloned.1.call-done.w3_ref = bf16[16,1024,512]{2,1,0:T(8,128)(2,1)} async-done(((bf16[1,1024,512]{2,1,0:T(8,128)(2,1)}), bf16[16,1024,512]{2,1,0:T(8,128)(2,1)}) %all-gather.23.cloned.1.call-update) | async-done | bytes 16777232 | tf_op jit(solution)/shard_map/all_gather | solution.py:136
  170.0 78.9 %all-gather.25.cloned.1.call-done.w2_ref = bf16[16,512,1024]{2,1,0:T(8,128)(2,1)} async-done(((bf16[1,512,1024]{2,1,0:T(8,128)(2,1)}), bf16[16,512,1024]{2,1,0:T(8,128)(2,1)}) %all-gather.25.cloned.1.call-update) | async-done | bytes 16777232 | tf_op jit(solution)/shard_map/all_gather | solution.py:136
  249.0 2.5 broadcast_3_yin_ref_dxin_ref.2.yin_ref
  251.5 2.5 broadcast_3_yin_ref_dxin_ref.2.clone.dxin_ref
  254.0 135.8 %home.2 = (f32[1024,1024]{1,0:T(8,128)}, f32[1024,1024]{1,0:T(8,128)}) custom-call(f32[1024,32]{1,0:T(8,128)} %copy.46.gd_ref, bf16[1024,1024]{1,0:T(8,128)(2,1)} %x_ref.3, bf16[1024,1024]{1,0:T(8,128)(2,1)} %dy_ref.3, bf16[16,1024,512]{2,1,0:T(8,128)(2,1)} %all-gather.21.cloned.1.call-done.w1_ref, ...), custom_call_target="tpu_custom_call", output_to_operand_aliasing={{0}: (6, {}), {1}: (7, {})} | custom-call | flops 103079215104 | bytes 50331648 | tf_op jit(solution)/shard_map/home/pallas_call | solution.py:77
  389.9 16.6 %all-gather.17.cloned.1.call-done.w3_ref = bf16[16,1024,512]{2,1,0:T(8,128)(2,1)} async-done(((bf16[1,1024,512]{2,1,0:T(8,128)(2,1)}), bf16[16,1024,512]{2,1,0:T(8,128)(2,1)}) %all-gather.17.cloned.1.call-update) | async-done | bytes 16777232 | tf_op jit(solution)/shard_map/all_gather | solution.py:136
  406.5 78.2 %all-gather.19.cloned.1.call-done.w2_ref = bf16[16,512,1024]{2,1,0:T(8,128)(2,1)} async-done(((bf16[1,512,1024]{2,1,0:T(8,128)(2,1)}), bf16[16,512,1024]{2,1,0:T(8,128)(2,1)}) %all-gather.19.cloned.1.call-update) | async-done | bytes 16777232 | tf_op jit(solution)/shard_map/all_gather | solution.py:136
  484.7 135.8 %home.3 = (f32[1024,1024]{1,0:T(8,128)}, f32[1024,1024]{1,0:T(8,128)}) custom-call(f32[1024,32]{1,0:T(8,128)} %copy.46.gd_ref, bf16[1024,1024]{1,0:T(8,128)(2,1)} %x_ref.3, bf16[1024,1024]{1,0:T(8,128)(2,1)} %dy_ref.3, bf16[16,1024,512]{2,1,0:T(8,128)(2,1)} %all-gather.15.cloned.1.call-done.w1_ref, ...), custom_call_target="tpu_custom_call", output_to_operand_aliasing={{0}: (6, {}), {1}: (7, {})} | custom-call | flops 103079215104 | bytes 50331648 | tf_op jit(solution)/shard_map/home/pallas_call | solution.py:77
  620.5 4.0 convert_element_type.10
  626.2 2.5 broadcast_2_i1_ref_i3_ref.2.i1_ref
  628.7 2.5 broadcast_2_i1_ref_i3_ref.2.clone.i3_ref
  631.3 2.5 broadcast_in_dim.20.i2_ref
  633.8 73.5 %owner.4 = (f32[2,1024,512]{2,1,0:T(8,128)}, f32[2,1024,512]{2,1,0:T(8,128)}, f32[2,512,1024]{2,1,0:T(8,128)}) custom-call(f32[4096,2]{1,0:T(8,128)} %bitcast.10, bf16[4096,1024]{1,0:T(8,128)(2,1)} %all-gather.39.cloned.1.call-done.x_ref, ...), custom_call_target="tpu_custom_call", output_to_operand_aliasing={{0}: (6, {}), {1}: (7, {}), {2}: (8, {})} | custom-call | flops 51539607552 | bytes 16777216 | tf_op jit(solution)/shard_map/owner/pallas_call | solution.py:116
  707.3 73.7 %owner.5 = (f32[2,1024,512]{2,1,0:T(8,128)}, f32[2,1024,512]{2,1,0:T(8,128)}, f32[2,512,1024]{2,1,0:T(8,128)}) custom-call(f32[4096,2]{1,0:T(8,128)} %bitcast.9, bf16[4096,1024]{1,0:T(8,128)(2,1)} %all-gather.35.cloned.1.call-done.x_ref, ...), custom_call_target="tpu_custom_call", output_to_operand_aliasing={{0}: (6, {}), {1}: (7, {}), {2}: (8, {})} | custom-call | flops 51539607552 | bytes 16777216 | tf_op jit(solution)/shard_map/owner/pallas_call | solution.py:116
  781.1 8.9 all-gather.33.cloned.1.call-done.dy_ref
  789.9 73.5 %owner.6 = (f32[2,1024,512]{2,1,0:T(8,128)}, f32[2,1024,512]{2,1,0:T(8,128)}, f32[2,512,1024]{2,1,0:T(8,128)}) custom-call(f32[4096,2]{1,0:T(8,128)} %bitcast.8, bf16[4096,1024]{1,0:T(8,128)(2,1)} %all-gather.31.cloned.1.call-done.x_ref, ...), custom_call_target="tpu_custom_call", output_to_operand_aliasing={{0}: (6, {}), {1}: (7, {}), {2}: (8, {})} | custom-call | flops 51539607552 | bytes 16777216 | tf_op jit(solution)/shard_map/owner/pallas_call | solution.py:116
  863.4 28.2 %all-gather.29.cloned.1.call-done.dy_ref = bf16[4096,1024]{1,0:T(8,128)(2,1)} async-done(((bf16[256,1024]{1,0:T(8,128)(2,1)}), bf16[4096,1024]{1,0:T(8,128)(2,1)}) %all-gather.29.cloned.1.call-update) | async-done | bytes 8388624 | tf_op jit(solution)/shard_map/all_gather | solution.py:136
  891.6 73.5 %owner.7 = (f32[2,1024,512]{2,1,0:T(8,128)}, f32[2,1024,512]{2,1,0:T(8,128)}, f32[2,512,1024]{2,1,0:T(8,128)}) custom-call(f32[4096,2]{1,0:T(8,128)} %bitcast.7, bf16[4096,1024]{1,0:T(8,128)(2,1)} %all-gather.27.cloned.1.call-done.x_ref, ...), custom_call_target="tpu_custom_call", output_to_operand_aliasing={{0}: (6, {}), {1}: (7, {}), {2}: (8, {})} | custom-call | flops 51539607552 | bytes 16777216 | tf_op jit(solution)/shard_map/owner/pallas_call | solution.py:116
  (57 shorter events, 19.7 us)
Async XLA Ops:
  7.2 3.3 copy-start.2
  7.2 82.5 %all-gather.21.cloned.1.call-start = ((), (), s32[]{:S(2)}) async-start(), calls=%async_computation.4 | async-start | bytes 17825792 | tf_op jit(solution)/shard_map/all_gather | solution.py:136
  10.4 159.7 %all-gather.23.cloned.1.call-start = ((), (), s32[]{:S(2)}) async-start(), calls=%async_computation.5 | async-start | bytes 17825792 | tf_op jit(solution)/shard_map/all_gather | solution.py:136
  11.9 77.8 %copy-start.1 = (bf16[1024,1024]{1,0:T(8,128)(2,1)S(1)}, bf16[1024,1024]{1,0:T(8,128)(2,1)}, u32[]{:S(2)}) copy-start(bf16[1024,1024]{1,0:T(8,128)(2,1)} %x_ref.3) | copy-start | bytes 6291460
  11.9 237.0 %all-gather.25.cloned.1.call-start = ((), (), s32[]{:S(2)}) async-start(), calls=%async_computation.6 | async-start | bytes 17825792 | tf_op jit(solution)/shard_map/all_gather | solution.py:136
  15.2 374.7 %all-gather.15.cloned.1.call-start = ((), (), s32[]{:S(2)}) async-start(), calls=%async_computation.1 | async-start | bytes 17825792 | tf_op jit(solution)/shard_map/all_gather | solution.py:136
  15.8 390.7 %all-gather.17.cloned.1.call-start = ((), (), s32[]{:S(2)}) async-start(), calls=%async_computation.2 | async-start | bytes 17825792 | tf_op jit(solution)/shard_map/all_gather | solution.py:136
  16.4 468.3 %all-gather.19.cloned.1.call-start = ((), (), s32[]{:S(2)}) async-start(), calls=%async_computation.3 | async-start | bytes 17825792 | tf_op jit(solution)/shard_map/all_gather | solution.py:136
  16.9 609.2 %all-gather.39.cloned.1.call-start = ((), (), s32[]{:S(2)}) async-start(), calls=%async_computation.13 | async-start | bytes 8912896 | tf_op jit(solution)/shard_map/all_gather | solution.py:136
  91.1 6.4 copy-start.4
  91.1 6.4 copy-start.3
  91.1 535.1 %all-gather.41.cloned.1.call-start = ((), (), s32[]{:S(2)}) async-start(), calls=%async_computation.14 | async-start | bytes 8912896 | tf_op jit(solution)/shard_map/all_gather | solution.py:136
  94.1 613.2 %all-gather.35.cloned.1.call-start = ((), (), s32[]{:S(2)}) async-start(), calls=%async_computation.11 | async-start | bytes 8912896 | tf_op jit(solution)/shard_map/all_gather | solution.py:136
  94.8 612.5 %all-gather.37.cloned.1.call-start = ((), (), s32[]{:S(2)}) async-start(), calls=%async_computation.12 | async-start | bytes 8912896 | tf_op jit(solution)/shard_map/all_gather | solution.py:136
  95.4 685.7 %all-gather.31.cloned.1.call-start = ((), (), s32[]{:S(2)}) async-start(), calls=%async_computation.9 | async-start | bytes 8912896 | tf_op jit(solution)/shard_map/all_gather | solution.py:136
  96.1 693.8 %all-gather.33.cloned.1.call-start = ((), (), s32[]{:S(2)}) async-start(), calls=%async_computation.10 | async-start | bytes 8912896 | tf_op jit(solution)/shard_map/all_gather | solution.py:136
  96.7 766.7 %all-gather.27.cloned.1.call-start = ((), (), s32[]{:S(2)}) async-start(), calls=%async_computation.7 | async-start | bytes 8912896 | tf_op jit(solution)/shard_map/all_gather | solution.py:136
  98.3 10.4 %all-to-all-start = ((f32[16,1024,2]{1,2,0:T(2,128)}), f32[16,1024,2]{1,2,0:T(2,128)S(1)}, u32[]{:S(2)}, u32[]{:S(2)}) async-start(f32[16,1024,2]{1,2,0:T(2,128)} %bitcast), calls=%async_computation | async-start | bytes 262144 | tf_op jit(solution)/shard_map/all_to_all | solution.py:139
  100.8 790.8 %all-gather.29.cloned.1.call-start = ((), (), s32[]{:S(2)}) async-start(), calls=%async_computation.8 | async-start | bytes 8912896 | tf_op jit(solution)/shard_map/all_gather | solution.py:136
  620.5 4.0 copy-start
Sparse Core Ops, SparseCore 0:
  10.8 78.8 all-gather.20
  92.5 77.4 all-gather.22
  172.9 76.0 all-gather.24
  251.6 76.0 all-gather.14
  330.4 76.0 all-gather.16
  408.6 76.0 all-gather.18
  486.9 48.6 all-gather.38
  537.9 48.6 all-gather.40
  588.8 48.6 all-gather.34
  639.6 48.6 all-gather.36
  690.5 48.6 all-gather.30
  741.3 48.6 all-gather.32
  792.2 48.6 all-gather.26
  843.0 48.6 all-gather.28

commit v2 on v1

v2 whole, which is shorter than its diff:
```python
import functools

import jax
import jax.numpy as jnp
from jax import lax
from jax.experimental import pallas as pl
from jax.experimental.pallas import tpu as pltpu
from jax.sharding import PartitionSpec as P

F32 = jnp.float32
BF = jnp.bfloat16
MESH = pl.DeviceIdType.MESH
NT = (((1,), (1,)), ((), ()))
TN = (((0,), (0,)), ((), ()))
BITS = (2, 4, 8)

ROUNDS = (
    lambda l: (l, ()),
    lambda l: ((l + 2) % 3, ()),
    lambda l: ((l + 1) % 3, ()),
    lambda l: ((l + 2) % 3, ((l + 2) % 3,)),
    lambda l: ((l + 1) % 3, ((l + 1) % 3,)),
    lambda l: ((l + 1) % 3, ((l + 2) % 3,)),
    lambda l: ((l + 1) % 3, ((l + 1) % 3, (l + 2) % 3)),
)
WROUNDS = ([(0, r) for r in range(3)] + [(1, r) for r in range(3)] + [(0, r) for r in range(3, 6)]
           + [(1, r) for r in range(3, 6)] + [(0, 6), (1, 6)])
SERVICE = {
    ('t', 0): (3, [('t', 3), ('t', 4)]),
    ('t', 1): (6, [('t', 5)]),
    ('t', 2): (6, []),
    ('t', 3): (9, [('t', 6), ('w', 0)]),
    ('t', 4): (11, [('w', 1)]),
    ('t', 5): (12, [('w', 2)]),
    ('t', 6): (15, [('w', 3)]),
    ('w', 0): (16, [('w', 4)]),
    ('w', 1): (18, [('w', 5)]),
    ('w', 2): (19, [('w', 6)]),
    ('w', 3): (22, [('w', 7)]),
    ('w', 4): (24, [('w', 8)]),
    ('w', 5): (26, [('w', 9)]),
    ('w', 6): (30, [('w', 10)]),
    ('w', 7): (32, [('w', 11)]),
    ('w', 8): (32, [('w', 12)]),
    ('w', 9): (36, [('w', 13)]),
    ('w', 10): (38, []),
    ('w', 11): (38, []),
    ('w', 12): (42, []),
    ('w', 13): (45, []),
}
PASSED = {8: [('t', r) for r in range(3)], 14: [('t', r) for r in range(3, 6)], 18: [('t', 6)],
          22: [('w', r) for r in range(3)], 28: [('w', r) for r in range(3, 6)], 34: [('w', r) for r in range(6, 9)],
          40: [('w', r) for r in range(9, 12)], 44: [('w', 12)], 46: [('w', 13)]}
TSTART = (0, 1, 2, 8)
WSTART = (0, 4, 10, 16, 22)
STEPS = 48


def _dot(a, b):
    return jnp.dot(a, b, preferred_element_type=F32)


def _dot_nt(a, b):
    return lax.dot_general(a, b, NT, preferred_element_type=F32)


def _dot_tn(a, b):
    return lax.dot_general(a, b, TN, preferred_element_type=F32)


def _column(gd, e):
    lane = lax.broadcasted_iota(jnp.int32, gd.shape, 1)
    return jnp.sum(jnp.where(lane == e, gd, 0.0), axis=1, keepdims=True)


def _inner(x, dy, g, w1, w3, w2):
    on = g > 0.0
    u = _dot(x, w1)
    v = _dot(x, w3)
    sig = jax.nn.sigmoid(u)
    su = u * sig
    do = (g * dy.astype(F32)).astype(BF)
    da = _dot_nt(do, w2)
    act = jnp.where(on, su * v, 0.0).astype(BF)
    du = jnp.where(on, da * v * (sig * (1.0 + u * (1.0 - sig))), 0.0).astype(BF)
    dv = jnp.where(on, da * su, 0.0).astype(BF)
    return act, do, du, dv


def _flip(dev, bit):
    return dev + bit * (1 - 2 * ((dev // bit) % 2))


def _cross(dev, links):
    for l in links:
        dev = _flip(dev, BITS[l])
    return dev


def _source(me, j, c):
    m = j + jnp.where(j == 3, 1, 0) - jnp.where(j == 4, 1, 0)
    dev = me
    for i, on in enumerate((c, m % 2, (m // 2) % 2, m // 4)):
        bit = 2 ** i
        dev = dev + on * bit * (1 - 2 * ((me // bit) % 2))
    return dev


def _group(q, base):
    return base + q % 3, q // 3


def _kernel(el, thirds, x_ref, dy_ref, w1_ref, w3_ref, w2_ref, gd_ref, gm_ref,
            y_ref, dx_ref, d1_ref, d3_ref, d2_ref, xa, dya, wa1, wa3, wa2,
            tx, tdy, tg, v1, v3, v2, o1, o3, o2, ox, ody, og, yacc, dxacc, a1, a3, a2,
            ts, tr, ws, wr, tps, tpr, wps, wpr, tos, tor, wos, wor, tl_sem, wl_sem, own_sem, out_sem):
    me = lax.axis_index('ep')
    other = _flip(me, 1)
    near = [_flip(me, b) for b in BITS]

    def remote(src, dst, ssem, rsem, dev):
        return pltpu.make_async_remote_copy(src_ref=src, dst_ref=dst, send_sem=ssem, recv_sem=rsem,
                                            device_id=(dev,), device_id_type=MESH)

    def pieces(kind, r, p, dev, mine, k):
        if kind == 't':
            rows = pl.ds(*thirds[p])
            return [((x_ref if mine else xa.at[dev]).at[rows], xa.at[dev, rows], (r, k, 0)),
                    ((dy_ref if mine else dya.at[dev]).at[rows], dya.at[dev, rows], (r, k, 1))]
        slot = WROUNDS[r][0]
        own, far = ((w1_ref, wa1), (w3_ref, wa3), (w2_ref, wa2))[p]
        return [(own.at[slot] if mine else far.at[dev * el + slot], far.at[dev * el + slot], (r, k))]

    def item_round(kind, r):
        return r if kind == 't' else WROUNDS[r][1]

    def sent(kind, r):
        ss, rs = (ts, tr) if kind == 't' else (ws, wr)
        out = []
        for l in range(3):
            p, path = ROUNDS[item_round(kind, r)](l)
            for src, dst, i in pieces(kind, r, p, _cross(me, path), not path, l):
                out.append(remote(src, dst, ss.at[i], rs.at[i], near[l]))
        return out

    def arrived(kind, r, at, ss, rs, dev):
        out = []
        for l in range(3):
            p, path = ROUNDS[item_round(kind, r)](l)
            for _, dst, i in pieces(kind, r, p, _cross(at, path + (l,)), False, l):
                out.append(remote(dst, dst, ss.at[i], rs.at[i], near[l] if dev is None else dev))
        return out

    def received(kind, r):
        return arrived(kind, r, me, *((ts, tr) if kind == 't' else (ws, wr)), None)

    def passed(kind, r):
        return arrived(kind, r, me, *((tps, tpr) if kind == 't' else (wps, wpr)), other)

    def passed_here(kind, r):
        return arrived(kind, r, other, *((tps, tpr) if kind == 't' else (wps, wpr)), other)

    def own_pass_t(dev):
        return [remote(x_ref, xa.at[dev], tos.at[0], tor.at[0], other),
                remote(dy_ref, dya.at[dev], tos.at[1], tor.at[1], other)]

    def own_pass_w(dev):
        return [remote(own.at[s], far.at[dev * el + s], wos.at[s, i], wor.at[s, i], other)
                for s in range(el) for i, (own, far) in enumerate(((w1_ref, wa1), (w3_ref, wa3), (w2_ref, wa2)))]

    def start(copies):
        for c in copies:
            c.start()

    own_loads = [pltpu.make_async_copy(a, b, own_sem.at[i]) for i, (a, b) in enumerate((
        (x_ref, ox), (dy_ref, ody), (gd_ref, og), (w1_ref, o1), (w3_ref, o3), (w2_ref, o2)))]
    start(own_loads)

    barrier = pltpu.get_barrier_semaphore()
    for dev in near + [other]:
        pl.semaphore_signal(barrier, inc=1, device_id=(dev,), device_id_type=MESH)
    pl.semaphore_wait(barrier, 4)
    for r in range(3):
        start(sent('t', r))
    start(own_pass_t(me))
    start(own_pass_w(me))

    yacc[...] = jnp.zeros_like(yacc)
    dxacc[...] = jnp.zeros_like(dxacc)
    a1[...] = jnp.zeros_like(a1)
    a3[...] = jnp.zeros_like(a3)
    a2[...] = jnp.zeros_like(a2)
    for c in own_loads:
        c.wait()

    def t_source(k):
        near_j, near_c = _group(k - 2, 1)
        mid_j, mid_c = _group(k - 8, 4)
        j = jnp.where(k < 2, 0, jnp.where(k < 8, near_j, jnp.where(k < 14, mid_j, 7)))
        c = jnp.where(k < 2, k, jnp.where(k < 8, near_c, jnp.where(k < 14, mid_c, k - 14)))
        return _source(me, j, c)

    def w_source(k):
        q = k - 4
        g = q // 6
        gj, gc = _group(q % 6, jnp.where(g < 2, 1, 4))
        j = jnp.where(k < 4, 0, jnp.where(k < 28, gj, 7))
        c = jnp.where(k < 4, k // 2, jnp.where(k < 28, gc, k % 2))
        slot = jnp.where(k < 4, k % 2, jnp.where(k < 28, g % 2, (k - 28) // 2))
        return _source(me, j, c) * el + slot

    def t_load(k, own):
        b = k % 2
        dev = t_source(k)
        return [pltpu.make_async_copy(x_ref if own else xa.at[dev], tx.at[b], tl_sem.at[b, 0]),
                pltpu.make_async_copy(dy_ref if own else dya.at[dev], tdy.at[b], tl_sem.at[b, 1]),
                pltpu.make_async_copy(gm_ref.at[dev], tg.at[b], tl_sem.at[b, 2])]

    def w_load(k, own):
        b = k % 2
        e = w_source(k)
        s = k % 2
        return [pltpu.make_async_copy(w1_ref.at[s] if own else wa1.at[e], v1.at[b], wl_sem.at[b, 0]),
                pltpu.make_async_copy(w3_ref.at[s] if own else wa3.at[e], v3.at[b], wl_sem.at[b, 1]),
                pltpu.make_async_copy(w2_ref.at[s] if own else wa2.at[e], v2.at[b], wl_sem.at[b, 2])]

    def fetch(load, k, owned):
        @pl.when(k < owned)
        def _():
            start(load(k, True))

        @pl.when(k >= owned)
        def _():
            start(load(k, False))

    def any_of(k, values):
        hit = k == values[0]
        for v in values[1:]:
            hit = jnp.logical_or(hit, k == v)
        return hit

    def turn(load, k, owned, starts, count):
        @pl.when(any_of(k, starts))
        def _():
            fetch(load, k, owned)

        @pl.when(jnp.logical_and(k + 1 < count, jnp.logical_not(any_of(k + 1, starts))))
        def _():
            fetch(load, k + 1, owned)

        for c in load(k, False):
            c.wait()

    @pl.loop(0, STEPS)
    def _(s):
        for key, (at, sends) in SERVICE.items():
            @pl.when(s == at)
            def _(key=key, sends=sends):
                for c in received(*key):
                    c.wait_recv()
                start(passed(*key))
                for k in sends:
                    start(sent(*k))

        @pl.when(s == 1)
        def _():
            for c in own_pass_t(other):
                c.wait_recv()

        @pl.when(s == 3)
        def _():
            for c in own_pass_w(other):
                c.wait_recv()

        for at, keys in PASSED.items():
            @pl.when(s == at)
            def _(keys=keys):
                for key in keys:
                    for c in passed_here(*key):
                        c.wait_recv()

        tokens = jnp.logical_or(s < 2, jnp.logical_and(s >= 6, s < 20))

        @pl.when(tokens)
        def _():
            k = jnp.where(s < 2, s, s - 4)
            b = k % 2
            turn(t_load, k, 1, TSTART, 16)

            @pl.loop(0, el)
            def _(e):
                x = tx[b]
                act, do, du, dv = _inner(x, tdy[b], _column(tg[b], e), o1[e], o3[e], o2[e])
                a1[e] += _dot_tn(x, du)
                a3[e] += _dot_tn(x, dv)
                a2[e] += _dot_tn(act, do)

        @pl.when(jnp.logical_not(tokens))
        def _():
            k = jnp.where(s < 6, s - 2, s - 16)
            b = k % 2
            turn(w_load, k, 2, WSTART, 32)
            g = _column(og[...], w_source(k))
            act, _, du, dv = _inner(ox[...], ody[...], g, v1[b], v3[b], v2[b])
            on = g > 0.0
            o = _dot(act, v2[b]).astype(BF).astype(F32)
            yacc[...] += jnp.where(on, g * o, 0.0)
            dxk = (_dot_nt(du, v1[b]) + _dot_nt(dv, v3[b])).astype(BF).astype(F32)
            dxacc[...] += jnp.where(on, dxk, 0.0)

        @pl.when(s == 20)
        def _():
            for i, (a, d) in enumerate(((a1, d1_ref), (a3, d3_ref), (a2, d2_ref))):
                pltpu.make_async_copy(a, d, out_sem.at[i]).start()

    tx[0] = yacc[...].astype(BF)
    tx[1] = dxacc[...].astype(BF)
    outs = [pltpu.make_async_copy(tx.at[0], y_ref, out_sem.at[3]), pltpu.make_async_copy(tx.at[1], dx_ref, out_sem.at[4])]
    start(outs)
    for i, (a, d) in enumerate(((a1, d1_ref), (a3, d3_ref), (a2, d2_ref))):
        pltpu.make_async_copy(a, d, out_sem.at[i]).wait()
    for key in SERVICE:
        for c in sent(*key) + passed(*key):
            c.wait_send()
    for c in own_pass_t(me) + own_pass_w(me):
        c.wait_send()
    for c in outs:
        c.wait()


def solution(mesh):
    n = mesh.shape['ep']

    def body(xl, rl, gl, dyl, w1l, w3l, w2l):
        tl, d = xl.shape
        el, _, ff = w1l.shape
        nexp = el * n
        hit = rl[:, :, None] == jnp.arange(nexp)[None, None, :]
        gd = jnp.sum(jnp.where(hit, gl.astype(F32)[:, :, None], 0.0), axis=1)
        gm = lax.all_to_all(gd.reshape(tl, n, el).transpose(1, 0, 2), 'ep', 0, 0, tiled=True)

        third = -(-tl // 48) * 16
        thirds = ((0, third), (third, (tl - third) // 2), ((tl + third) // 2, (tl - third) // 2))
        dma = pltpu.SemaphoreType.DMA
        out = lambda *s: jax.ShapeDtypeStruct(s, F32)
        outb = lambda *s: jax.ShapeDtypeStruct(s, BF)
        nw = len(WROUNDS)
        hbm = pl.BlockSpec(memory_space=pl.ANY)
        res = pl.pallas_call(
            functools.partial(_kernel, el, thirds),
            out_shape=[outb(tl, d), outb(tl, d), out(el, d, ff), out(el, d, ff), out(el, ff, d),
                       outb(n, tl, d), outb(n, tl, d), outb(nexp, d, ff), outb(nexp, d, ff), outb(nexp, ff, d)],
            in_specs=[hbm] * 7,
            out_specs=[hbm] * 10,
            scratch_shapes=[
                pltpu.VMEM((2, tl, d), BF), pltpu.VMEM((2, tl, d), BF), pltpu.VMEM((2, tl, el), F32),
                pltpu.VMEM((2, d, ff), BF), pltpu.VMEM((2, d, ff), BF), pltpu.VMEM((2, ff, d), BF),
                pltpu.VMEM((el, d, ff), BF), pltpu.VMEM((el, d, ff), BF), pltpu.VMEM((el, ff, d), BF),
                pltpu.VMEM((tl, d), BF), pltpu.VMEM((tl, d), BF), pltpu.VMEM((tl, nexp), F32),
                pltpu.VMEM((tl, d), F32), pltpu.VMEM((tl, d), F32),
                pltpu.VMEM((el, d, ff), F32), pltpu.VMEM((el, d, ff), F32), pltpu.VMEM((el, ff, d), F32),
                dma((7, 3, 2)), dma((7, 3, 2)), dma((nw, 3)), dma((nw, 3)),
                dma((7, 3, 2)), dma((7, 3, 2)), dma((nw, 3)), dma((nw, 3)),
                dma((2,)), dma((2,)), dma((el, 3)), dma((el, 3)),
                dma((2, 3)), dma((2, 3)), dma((6,)), dma((5,)),
            ],
            compiler_params=pltpu.CompilerParams(collective_id=0, has_side_effects=True, vmem_limit_bytes=67043328),
            name='moe',
        )(xl, dyl, w1l, w3l, w2l, gd, gm)
        return tuple(res[:5])

    spec_t = P('ep', None)
    spec_w = P('ep', None, None)
    return jax.shard_map(body, mesh=mesh, in_specs=(spec_t, spec_t, spec_t, spec_t, spec_w, spec_w, spec_w), out_specs=(spec_t, spec_t, spec_w, spec_w, spec_w), check_vma=False)
```

time: 972 us -> 604 us (0.62)
  waiting for transfers between devices: 349 us -> 5.09 us
  local copies, waits for them, and re-layouts: 34.5 us -> 20.4 us
  between operations: 14 us -> 0.67 us
    all_gather x14 -> x0, waiting for transfers between devices: 337 us -> none  [body(): gather = lambda a: lax.all_gather(a, 'ep', axis=0, tiled=True)]
    slice x10 -> x0, local copies, waits for them, and re-layouts: 20 us -> none  [the longest x5 8.01 us: body(): gt = mine[:, r].reshape(n * step, el)]
    unnamed x10 -> x13, local copies, waits for them, and re-layouts: 0.02 us -> 14 us
    another operation x4 -> x0, local copies, waits for them, and re-layouts: 10.2 us -> none
    pallas_call x6 -> x1, Pallas kernels: 566 us -> 570 us  [body(): pl.pallas_call(functools.partial(_kernel, el, thirds), out_shape=[outb(tl...]
  transfers between devices with their start and end apart: 15 -> 1, of which waited for: 8 -> 1; matrix products, arithmetic and copies ran while one was open for 4% -> 0% of each run, Pallas kernels for 51% -> 0%
where the time goes in v2:
time: 604 us; the launch traced here: 603 us
  Pallas kernels  570 us (94%)
  local copies, waits for them, and re-layouts  20.4 us (3%)
    pallas_call x1, Pallas kernels, body(): pl.pallas_call(functools.partial(_kernel, el, thirds), out_shape=[outb(tl...  570 us
    unnamed x13, local copies, waits for them, and re-layouts  14 us
  transfers between devices with their start and end apart: 1, of which 1 were waited for; matrix products, arithmetic and copies ran while one was open for 0% of the time, Pallas kernels for 0%

profile of v2, /device:TPU:0, one launch (start us, length us, event | category | flops | bytes accessed | tf_op | source)
XLA Modules:
  0.0 603.2 jit_solution(18052051225753101386)
XLA Ops:
  0.6 0.7 convert_element_type.3
  1.4 0.9 select_reduce_fusion
  2.2 0.7 reshape.15
  3.0 5.3 all-to-all-start
  8.3 1.0 copy.22.gd_ref
  9.3 5.1 all-to-all-done
  14.4 4.7 copy.23.gm_ref
  19.0 570.2 %moe.1 = (bf16[1024,1024]{1,0:T(8,128)(2,1)}, bf16[1024,1024]{1,0:T(8,128)(2,1)}, f32[2,1024,512]{2,1,0:T(8,128)}, f32[2,1024,512]{2,1,0:T(8,128)}, f32[2,512,10...) custom-call(bf16[1024,1024]{1,0:T(8,128)(2,1)} %x_ref.1, ...), custom_call_target="tpu_custom_call" | custom-call | tf_op jit(solution)/shard_map/moe/pallas_call | solution.py:349
  589.2 0.0 copy-start.3
  589.2 0.0 copy-start.2
  589.2 3.2 copy.29
  592.4 0.0 copy-done.3
  592.4 1.3 copy.30
  593.8 0.0 copy-done.2
  593.8 0.0 copy-start.1
  593.8 2.1 copy.31
  595.9 1.6 copy-done.1
  597.5 0.0 copy-start
  597.5 2.1 copy.32
  599.6 1.6 copy-done
  601.2 2.0 copy.33
Async XLA Ops:
  3.0 11.4 %all-to-all-start = ((f32[16,1024,2]{1,2,0:T(2,128)}), f32[16,1024,2]{1,2,0:T(2,128)S(1)}, u32[]{:S(2)}, u32[]{:S(2)}) async-start(f32[16,1024,2]{1,2,0:T(2,128)} %bitcast), calls=%async_computation | async-start | bytes 262144 | tf_op jit(solution)/shard_map/all_to_all | solution.py:340
  589.2 3.3 copy-start.3
  589.2 4.6 copy-start.2
  593.8 3.7 copy-start.1
  597.5 3.7 copy-start

commit v3 on v2

--- a/solution.py
+++ b/solution.py
@@ -23,6 +23,7 @@
     lambda l: ((l + 1) % 3, ((l + 2) % 3,)),
     lambda l: ((l + 1) % 3, ((l + 1) % 3, (l + 2) % 3)),
 )
+SPREAD = ((4, 3, 5), (3, 5, 4), (4, 3, 5))
 WROUNDS = ([(0, r) for r in range(3)] + [(1, r) for r in range(3)] + [(0, r) for r in range(3, 6)]
            + [(1, r) for r in range(3, 6)] + [(0, 6), (1, 6)])
 SERVICE = {
@@ -41,18 +42,18 @@
     ('w', 5): (26, [('w', 9)]),
     ('w', 6): (30, [('w', 10)]),
     ('w', 7): (32, [('w', 11)]),
-    ('w', 8): (32, [('w', 12)]),
-    ('w', 9): (36, [('w', 13)]),
-    ('w', 10): (38, []),
-    ('w', 11): (38, []),
-    ('w', 12): (42, []),
-    ('w', 13): (45, []),
+    ('w', 8): (34, [('w', 12)]),
+    ('w', 9): (38, []),
+    ('w', 10): (38, [('w', 13)]),
+    ('w', 11): (40, []),
+    ('w', 12): (44, []),
+    ('w', 13): (46, []),
 }
 PASSED = {8: [('t', r) for r in range(3)], 14: [('t', r) for r in range(3, 6)], 18: [('t', 6)],
-          22: [('w', r) for r in range(3)], 28: [('w', r) for r in range(3, 6)], 34: [('w', r) for r in range(6, 9)],
-          40: [('w', r) for r in range(9, 12)], 44: [('w', 12)], 46: [('w', 13)]}
+          22: [('w', r) for r in range(3)], 28: [('w', r) for r in range(3, 6)], 33: [('w', 6), ('w', 7)], 35: [('w', 8)],
+          39: [('w', 9), ('w', 10)], 41: [('w', 11)], 45: [('w', 12)], 47: [('w', 13)]}
 TSTART = (0, 1, 2, 8)
-WSTART = (0, 4, 10, 16, 22)
+WSTART = (0, 4, 10, 16, 17, 18, 22, 23, 24, 28, 29, 30, 31)
 STEPS = 48
 
 
@@ -110,8 +111,8 @@
     return base + q % 3, q // 3
 
 
-def _kernel(el, thirds, x_ref, dy_ref, w1_ref, w3_ref, w2_ref, gd_ref, gm_ref,
-            y_ref, dx_ref, d1_ref, d3_ref, d2_ref, xa, dya, wa1, wa3, wa2,
+def _kernel(el, thirds, x_ref, dy_ref, gt_ref, w1_ref, w3_ref, w2_ref,
+            y_ref, dx_ref, d1_ref, d3_ref, d2_ref, xa, dya, gta, wa1, wa3, wa2,
             tx, tdy, tg, v1, v3, v2, o1, o3, o2, ox, ody, og, yacc, dxacc, a1, a3, a2,
             ts, tr, ws, wr, tps, tpr, wps, wpr, tos, tor, wos, wor, tl_sem, wl_sem, own_sem, out_sem):
     me = lax.axis_index('ep')
@@ -125,20 +126,24 @@
     def pieces(kind, r, p, dev, mine, k):
         if kind == 't':
             rows = pl.ds(*thirds[p])
-            return [((x_ref if mine else xa.at[dev]).at[rows], xa.at[dev, rows], (r, k, 0)),
-                    ((dy_ref if mine else dya.at[dev]).at[rows], dya.at[dev, rows], (r, k, 1))]
+            gate = [(gt_ref if mine else gta.at[dev], gta.at[dev], (r, k, 2))] if p == 0 else []
+            return gate + [((x_ref if mine else xa.at[dev]).at[rows], xa.at[dev, rows], (r, k, 0)),
+                           ((dy_ref if mine else dya.at[dev]).at[rows], dya.at[dev, rows], (r, k, 1))]
         slot = WROUNDS[r][0]
         own, far = ((w1_ref, wa1), (w3_ref, wa3), (w2_ref, wa2))[p]
         return [(own.at[slot] if mine else far.at[dev * el + slot], far.at[dev * el + slot], (r, k))]
 
-    def item_round(kind, r):
-        return r if kind == 't' else WROUNDS[r][1]
+    def leg(kind, r, l):
+        i = r if kind == 't' else WROUNDS[r][1]
+        if kind == 'w' and 3 <= i < 6:
+            i = SPREAD[l][i - 3]
+        return ROUNDS[i](l)
 
     def sent(kind, r):
         ss, rs = (ts, tr) if kind == 't' else (ws, wr)
         out = []
         for l in range(3):
-            p, path = ROUNDS[item_round(kind, r)](l)
+            p, path = leg(kind, r, l)
             for src, dst, i in pieces(kind, r, p, _cross(me, path), not path, l):
                 out.append(remote(src, dst, ss.at[i], rs.at[i], near[l]))
         return out
@@ -146,7 +151,7 @@
     def arrived(kind, r, at, ss, rs, dev):
         out = []
         for l in range(3):
-            p, path = ROUNDS[item_round(kind, r)](l)
+            p, path = leg(kind, r, l)
             for _, dst, i in pieces(kind, r, p, _cross(at, path + (l,)), False, l):
                 out.append(remote(dst, dst, ss.at[i], rs.at[i], near[l] if dev is None else dev))
         return out
@@ -162,7 +167,8 @@
 
     def own_pass_t(dev):
         return [remote(x_ref, xa.at[dev], tos.at[0], tor.at[0], other),
-                remote(dy_ref, dya.at[dev], tos.at[1], tor.at[1], other)]
+                remote(dy_ref, dya.at[dev], tos.at[1], tor.at[1], other),
+                remote(gt_ref, gta.at[dev], tos.at[2], tor.at[2], other)]
 
     def own_pass_w(dev):
         return [remote(own.at[s], far.at[dev * el + s], wos.at[s, i], wor.at[s, i], other)
@@ -173,7 +179,7 @@
             c.start()
 
     own_loads = [pltpu.make_async_copy(a, b, own_sem.at[i]) for i, (a, b) in enumerate((
-        (x_ref, ox), (dy_ref, ody), (gd_ref, og), (w1_ref, o1), (w3_ref, o3), (w2_ref, o2)))]
+        (x_ref, ox), (dy_ref, ody), (gt_ref, tg.at[1]), (w1_ref, o1), (w3_ref, o3), (w2_ref, o2)))]
     start(own_loads)
 
     barrier = pltpu.get_barrier_semaphore()
@@ -192,6 +198,7 @@
     a2[...] = jnp.zeros_like(a2)
     for c in own_loads:
         c.wait()
+    og[...] = jnp.transpose(tg[1].astype(F32))
 
     def t_source(k):
         near_j, near_c = _group(k - 2, 1)
@@ -203,7 +210,9 @@
     def w_source(k):
         q = k - 4
         g = q // 6
-        gj, gc = _group(q % 6, jnp.where(g < 2, 1, 4))
+        i = q % 6
+        gj = jnp.where(g < 2, 1 + i % 3, jnp.where(i < 2, 4, 5 + i % 2))
+        gc = jnp.where(g < 2, i // 3, jnp.where(i < 2, i, i // 2 - 1))
         j = jnp.where(k < 4, 0, jnp.where(k < 28, gj, 7))
         c = jnp.where(k < 4, k // 2, jnp.where(k < 28, gc, k % 2))
         slot = jnp.where(k < 4, k % 2, jnp.where(k < 28, g % 2, (k - 28) // 2))
@@ -214,7 +223,7 @@
         dev = t_source(k)
         return [pltpu.make_async_copy(x_ref if own else xa.at[dev], tx.at[b], tl_sem.at[b, 0]),
                 pltpu.make_async_copy(dy_ref if own else dya.at[dev], tdy.at[b], tl_sem.at[b, 1]),
-                pltpu.make_async_copy(gm_ref.at[dev], tg.at[b], tl_sem.at[b, 2])]
+                pltpu.make_async_copy(gt_ref if own else gta.at[dev], tg.at[b], tl_sem.at[b, 2])]
 
     def w_load(k, own):
         b = k % 2
@@ -290,7 +299,7 @@
             @pl.loop(0, el)
             def _(e):
                 x = tx[b]
-                act, do, du, dv = _inner(x, tdy[b], _column(tg[b], e), o1[e], o3[e], o2[e])
+                act, do, du, dv = _inner(x, tdy[b], _column(jnp.transpose(tg[b].astype(F32)), me * el + e), o1[e], o3[e], o2[e])
                 a1[e] += _dot_tn(x, du)
                 a3[e] += _dot_tn(x, dv)
                 a2[e] += _dot_tn(act, do)
@@ -335,9 +344,8 @@
         tl, d = xl.shape
         el, _, ff = w1l.shape
         nexp = el * n
-        hit = rl[:, :, None] == jnp.arange(nexp)[None, None, :]
-        gd = jnp.sum(jnp.where(hit, gl.astype(F32)[:, :, None], 0.0), axis=1)
-        gm = lax.all_to_all(gd.reshape(tl, n, el).transpose(1, 0, 2), 'ep', 0, 0, tiled=True)
+        hit = rl.T[None] == jnp.arange(nexp)[:, None, None]
+        gt = jnp.sum(jnp.where(hit, gl.T.astype(F32)[None], 0.0), axis=1).astype(BF)
 
         third = -(-tl // 48) * 16
         thirds = ((0, third), (third, (tl - third) // 2), ((tl + third) // 2, (tl - third) // 2))
@@ -349,24 +357,24 @@
         res = pl.pallas_call(
             functools.partial(_kernel, el, thirds),
             out_shape=[outb(tl, d), outb(tl, d), out(el, d, ff), out(el, d, ff), out(el, ff, d),
-                       outb(n, tl, d), outb(n, tl, d), outb(nexp, d, ff), outb(nexp, d, ff), outb(nexp, ff, d)],
-            in_specs=[hbm] * 7,
-            out_specs=[hbm] * 10,
+                       outb(n, tl, d), outb(n, tl, d), outb(n, nexp, tl), outb(nexp, d, ff), outb(nexp, d, ff), outb(nexp, ff, d)],
+            in_specs=[hbm] * 6,
+            out_specs=[hbm] * 11,
             scratch_shapes=[
-                pltpu.VMEM((2, tl, d), BF), pltpu.VMEM((2, tl, d), BF), pltpu.VMEM((2, tl, el), F32),
+                pltpu.VMEM((2, tl, d), BF), pltpu.VMEM((2, tl, d), BF), pltpu.VMEM((2, nexp, tl), BF),
                 pltpu.VMEM((2, d, ff), BF), pltpu.VMEM((2, d, ff), BF), pltpu.VMEM((2, ff, d), BF),
                 pltpu.VMEM((el, d, ff), BF), pltpu.VMEM((el, d, ff), BF), pltpu.VMEM((el, ff, d), BF),
                 pltpu.VMEM((tl, d), BF), pltpu.VMEM((tl, d), BF), pltpu.VMEM((tl, nexp), F32),
                 pltpu.VMEM((tl, d), F32), pltpu.VMEM((tl, d), F32),
                 pltpu.VMEM((el, d, ff), F32), pltpu.VMEM((el, d, ff), F32), pltpu.VMEM((el, ff, d), F32),
-                dma((7, 3, 2)), dma((7, 3, 2)), dma((nw, 3)), dma((nw, 3)),
-                dma((7, 3, 2)), dma((7, 3, 2)), dma((nw, 3)), dma((nw, 3)),
-                dma((2,)), dma((2,)), dma((el, 3)), dma((el, 3)),
+                dma((7, 3, 3)), dma((7, 3, 3)), dma((nw, 3)), dma((nw, 3)),
+                dma((7, 3, 3)), dma((7, 3, 3)), dma((nw, 3)), dma((nw, 3)),
+                dma((3,)), dma((3,)), dma((el, 3)), dma((el, 3)),
                 dma((2, 3)), dma((2, 3)), dma((6,)), dma((5,)),
             ],
             compiler_params=pltpu.CompilerParams(collective_id=0, has_side_effects=True, vmem_limit_bytes=67043328),
             name='moe',
-        )(xl, dyl, w1l, w3l, w2l, gd, gm)
+        )(xl, dyl, gt, w1l, w3l, w2l)
         return tuple(res[:5])
 
     spec_t = P('ep', None)

time: 604 us -> 589 us (0.975)
  local copies, waits for them, and re-layouts: 20.4 us -> 14 us
  transfers between devices with their start and end apart: 1 -> 0, of which waited for: 1 -> 0; matrix products, arithmetic and copies ran while one was open for 0% -> 0% of each run, Pallas kernels for 0% -> 0%
where the time goes in v3:
time: 589 us; the launch traced here: 588 us
  Pallas kernels  571 us (97%)
  local copies, waits for them, and re-layouts  14 us (2%)
    pallas_call x1, Pallas kernels, body(): pl.pallas_call(functools.partial(_kernel, el, thirds), out_shape=[outb(tl...  571 us
    unnamed x13, local copies, waits for them, and re-layouts  14 us

profile of v3, /device:TPU:0, one launch (start us, length us, event | category | flops | bytes accessed | tf_op | source)
XLA Modules:
  0.0 588.1 jit_solution(17705032692743873834)
XLA Ops:
  0.6 0.7 convert_bitcast_fusion
  1.4 1.7 select_reduce_fusion.gt_ref
  3.1 571.0 %moe.1 = (bf16[1024,1024]{1,0:T(8,128)(2,1)}, bf16[1024,1024]{1,0:T(8,128)(2,1)}, f32[2,1024,512]{2,1,0:T(8,128)}, f32[2,1024,512]{2,1,0:T(8,128)}, f32[2,512,10...) custom-call(bf16[1024,1024]{1,0:T(8,128)(2,1)} %x_ref.1, ...), custom_call_target="tpu_custom_call" | custom-call | tf_op jit(solution)/shard_map/moe/pallas_call | solution.py:357
  574.1 0.0 copy-start.3
  574.1 0.0 copy-start.2
  574.1 3.2 copy.17
  577.4 0.0 copy-done.3
  577.4 1.3 copy.18
  578.7 0.0 copy-done.2
  578.7 0.0 copy-start.1
  578.7 2.1 copy.19
  580.8 1.6 copy-done.1
  582.4 0.0 copy-start
  582.4 2.1 copy.20
  584.5 1.6 copy-done
  586.1 2.0 copy.21
Async XLA Ops:
  574.1 3.3 copy-start.3
  574.1 4.6 copy-start.2
  578.7 3.7 copy-start.1
  582.4 3.7 copy-start

commit v4 on v3

--- a/solution.py
+++ b/solution.py
@@ -47,14 +47,14 @@
     ('w', 10): (38, [('w', 13)]),
     ('w', 11): (40, []),
     ('w', 12): (44, []),
-    ('w', 13): (46, []),
 }
+LAST = ('w', 13)
 PASSED = {8: [('t', r) for r in range(3)], 14: [('t', r) for r in range(3, 6)], 18: [('t', 6)],
           22: [('w', r) for r in range(3)], 28: [('w', r) for r in range(3, 6)], 33: [('w', 6), ('w', 7)], 35: [('w', 8)],
-          39: [('w', 9), ('w', 10)], 41: [('w', 11)], 45: [('w', 12)], 47: [('w', 13)]}
+          39: [('w', 9), ('w', 10)], 41: [('w', 11)], 45: [('w', 12)]}
 TSTART = (0, 1, 2, 8)
-WSTART = (0, 4, 10, 16, 17, 18, 22, 23, 24, 28, 29, 30, 31)
-STEPS = 48
+WSTART = (0, 4, 10, 16, 17, 18, 22, 23, 24, 28, 29)
+STEPS = 46
 
 
 def _dot(a, b):
@@ -88,6 +88,14 @@
     return act, do, du, dv
 
 
+def _expert(x, dy, g, w1, w3, w2):
+    act, _, du, dv = _inner(x, dy, g, w1, w3, w2)
+    on = g > 0.0
+    o = _dot(act, w2).astype(BF).astype(F32)
+    dxk = (_dot_nt(du, w1) + _dot_nt(dv, w3)).astype(BF).astype(F32)
+    return jnp.where(on, g * o, 0.0), jnp.where(on, dxk, 0.0)
+
+
 def _flip(dev, bit):
     return dev + bit * (1 - 2 * ((dev // bit) % 2))
 
@@ -112,7 +120,7 @@
 
 
 def _kernel(el, thirds, x_ref, dy_ref, gt_ref, w1_ref, w3_ref, w2_ref,
-            y_ref, dx_ref, d1_ref, d3_ref, d2_ref, xa, dya, gta, wa1, wa3, wa2,
+            yf_ref, dxf_ref, d1_ref, d3_ref, d2_ref, xa, dya, gta, wa1, wa3, wa2,
             tx, tdy, tg, v1, v3, v2, o1, o3, o2, ox, ody, og, yacc, dxacc, a1, a3, a2,
             ts, tr, ws, wr, tps, tpr, wps, wpr, tos, tor, wos, wor, tl_sem, wl_sem, own_sem, out_sem):
     me = lax.axis_index('ep')
@@ -126,7 +134,7 @@
     def pieces(kind, r, p, dev, mine, k):
         if kind == 't':
             rows = pl.ds(*thirds[p])
-            gate = [(gt_ref if mine else gta.at[dev], gta.at[dev], (r, k, 2))] if p == 0 else []
+            gate = [(gt_ref if mine else gta.at[dev], gta.at[dev], (r, k, 2))] if p == 1 else []
             return gate + [((x_ref if mine else xa.at[dev]).at[rows], xa.at[dev, rows], (r, k, 0)),
                            ((dy_ref if mine else dya.at[dev]).at[rows], dya.at[dev, rows], (r, k, 1))]
         slot = WROUNDS[r][0]
@@ -308,33 +316,82 @@
         def _():
             k = jnp.where(s < 6, s - 2, s - 16)
             b = k % 2
-            turn(w_load, k, 2, WSTART, 32)
-            g = _column(og[...], w_source(k))
-            act, _, du, dv = _inner(ox[...], ody[...], g, v1[b], v3[b], v2[b])
-            on = g > 0.0
-            o = _dot(act, v2[b]).astype(BF).astype(F32)
-            yacc[...] += jnp.where(on, g * o, 0.0)
-            dxk = (_dot_nt(du, v1[b]) + _dot_nt(dv, v3[b])).astype(BF).astype(F32)
-            dxacc[...] += jnp.where(on, dxk, 0.0)
+            turn(w_load, k, 2, WSTART, 30)
+            yk, dxk = _expert(ox[...], ody[...], _column(og[...], w_source(k)), v1[b], v3[b], v2[b])
+            yacc[...] += yk
+            dxacc[...] += dxk
 
         @pl.when(s == 20)
         def _():
             for i, (a, d) in enumerate(((a1, d1_ref), (a3, d3_ref), (a2, d2_ref))):
                 pltpu.make_async_copy(a, d, out_sem.at[i]).start()
 
-    tx[0] = yacc[...].astype(BF)
-    tx[1] = dxacc[...].astype(BF)
-    outs = [pltpu.make_async_copy(tx.at[0], y_ref, out_sem.at[3]), pltpu.make_async_copy(tx.at[1], dx_ref, out_sem.at[4])]
+    outs = [pltpu.make_async_copy(yacc, yf_ref, out_sem.at[3]), pltpu.make_async_copy(dxacc, dxf_ref, out_sem.at[4])]
     start(outs)
+    for c in received(*LAST):
+        c.wait_recv()
+    start(passed(*LAST))
     for i, (a, d) in enumerate(((a1, d1_ref), (a3, d3_ref), (a2, d2_ref))):
         pltpu.make_async_copy(a, d, out_sem.at[i]).wait()
+    for key in list(SERVICE) + [LAST]:
+        for c in sent(*key):
+            c.wait_send()
     for key in SERVICE:
-        for c in sent(*key) + passed(*key):
+        for c in passed(*key):
             c.wait_send()
     for c in own_pass_t(me) + own_pass_w(me):
         c.wait_send()
     for c in outs:
         c.wait()
+    for c in passed_here(*LAST):
+        c.wait_recv()
+    for c in passed(*LAST):
+        c.wait_send()
+
+
+def _finish_kernel(el, x_ref, dy_ref, gt_ref, wa1, wa3, wa2, yf_ref, dxf_ref, e1_ref, e3_ref, e2_ref,
+                   y_ref, dx_ref, d1_ref, d3_ref, d2_ref,
+                   ox, ody, tg, v1, v3, v2, yacc, dxacc, yo, dxo, a1, a3, a2, in_sem, w_sem, acc_sem, d_sem, o_sem):
+    me = lax.axis_index('ep')
+    far = _cross(me, (0, 1, 2))
+    experts = [far * el + el - 1, _flip(far, 1) * el + el - 1]
+    copy = pltpu.make_async_copy
+
+    def begin(pairs, sem):
+        copies = [copy(a, b, sem.at[i]) for i, (a, b) in enumerate(pairs)]
+        for c in copies:
+            c.start()
+        return copies
+
+    def finish(copies):
+        for c in copies:
+            c.wait()
+
+    def weights(i):
+        e = experts[i]
+        return begin(((wa1.at[e], v1.at[i]), (wa3.at[e], v3.at[i]), (wa2.at[e], v2.at[i])), w_sem.at[i])
+
+    tokens = begin(((gt_ref, tg), (x_ref, ox), (dy_ref, ody)), in_sem)
+    first = weights(0)
+    finish(tokens)
+    finish(first)
+    acc = begin(((yf_ref, yacc), (dxf_ref, dxacc)), acc_sem)
+    second = weights(1)
+    grads = begin(((e1_ref, a1), (e3_ref, a3), (e2_ref, a2)), d_sem)
+    gd = jnp.transpose(tg[...].astype(F32))
+    yk, dxk = _expert(ox[...], ody[...], _column(gd, experts[0]), v1[0], v3[0], v2[0])
+    finish(acc)
+    yacc[...] += yk
+    dxacc[...] += dxk
+    finish(second)
+    finish(grads)
+    outs = begin(((a1, d1_ref), (a3, d3_ref), (a2, d2_ref)), o_sem)
+    yk, dxk = _expert(ox[...], ody[...], _column(gd, experts[1]), v1[1], v3[1], v2[1])
+    yo[...] = (yacc[...] + yk).astype(BF)
+    dxo[...] = (dxacc[...] + dxk).astype(BF)
+    last = begin(((yo, y_ref), (dxo, dx_ref)), in_sem)
+    finish(outs)
+    finish(last)
 
 
 def solution(mesh):
@@ -347,8 +404,8 @@
         hit = rl.T[None] == jnp.arange(nexp)[:, None, None]
         gt = jnp.sum(jnp.where(hit, gl.T.astype(F32)[None], 0.0), axis=1).astype(BF)
 
-        third = -(-tl // 48) * 16
-        thirds = ((0, third), (third, (tl - third) // 2), ((tl + third) // 2, (tl - third) // 2))
+        mid = tl // 48 * 16
+        thirds = ((0, (tl - mid) // 2), ((tl - mid) // 2, mid), ((tl + mid) // 2, (tl - mid) // 2))
         dma = pltpu.SemaphoreType.DMA
         out = lambda *s: jax.ShapeDtypeStruct(s, F32)
         outb = lambda *s: jax.ShapeDtypeStruct(s, BF)
@@ -356,7 +413,7 @@
         hbm = pl.BlockSpec(memory_space=pl.ANY)
         res = pl.pallas_call(
             functools.partial(_kernel, el, thirds),
-            out_shape=[outb(tl, d), outb(tl, d), out(el, d, ff), out(el, d, ff), out(el, ff, d),
+            out_shape=[out(tl, d), out(tl, d), out(el, d, ff), out(el, d, ff), out(el, ff, d),
                        outb(n, tl, d), outb(n, tl, d), outb(n, nexp, tl), outb(nexp, d, ff), outb(nexp, d, ff), outb(nexp, ff, d)],
             in_specs=[hbm] * 6,
             out_specs=[hbm] * 11,
@@ -375,7 +432,22 @@
             compiler_params=pltpu.CompilerParams(collective_id=0, has_side_effects=True, vmem_limit_bytes=67043328),
             name='moe',
         )(xl, dyl, gt, w1l, w3l, w2l)
-        return tuple(res[:5])
+        wa1, wa3, wa2 = res[8:]
+        return tuple(pl.pallas_call(
+            functools.partial(_finish_kernel, el),
+            out_shape=[outb(tl, d), outb(tl, d), out(el, d, ff), out(el, d, ff), out(el, ff, d)],
+            in_specs=[hbm] * 11,
+            out_specs=[hbm] * 5,
+            scratch_shapes=[
+                pltpu.VMEM((tl, d), BF), pltpu.VMEM((tl, d), BF), pltpu.VMEM((nexp, tl), BF),
+                pltpu.VMEM((2, d, ff), BF), pltpu.VMEM((2, d, ff), BF), pltpu.VMEM((2, ff, d), BF),
+                pltpu.VMEM((tl, d), F32), pltpu.VMEM((tl, d), F32), pltpu.VMEM((tl, d), BF), pltpu.VMEM((tl, d), BF),
+                pltpu.VMEM((el, d, ff), F32), pltpu.VMEM((el, d, ff), F32), pltpu.VMEM((el, ff, d), F32),
+                dma((3,)), dma((2, 3)), dma((2,)), dma((3,)), dma((3,)),
+            ],
+            compiler_params=pltpu.CompilerParams(vmem_limit_bytes=67043328),
+            name='finish',
+        )(xl, dyl, gt, wa1, wa3, wa2, *res[:5]))
 
     spec_t = P('ep', None)
     spec_w = P('ep', None, None)

time: 589 us -> 575 us (0.976)
  local copies, waits for them, and re-layouts: 14 us -> 0 us
    unnamed x13 -> x0, local copies, waits for them, and re-layouts: 14 us -> none
    pallas_call x1 -> x2, Pallas kernels: 571 us -> 571 us  [the longest x1 551 us: body(): pl.pallas_call(functools.partial(_kernel, el, thirds), out_shape=[out(tl,...]
where the time goes in v4:
time: 575 us
  Pallas kernels  571 us (99%)
    pallas_call x1, Pallas kernels, body(): pl.pallas_call(functools.partial(_kernel, el, thirds), out_shape=[out(tl,...  551 us
    pallas_call x1, Pallas kernels, body(): pl.pallas_call(functools.partial(_finish_kernel, el), out_shape=[outb(tl,...  19.9 us

profile of v4, /device:TPU:0, one launch (start us, length us, event | category | flops | bytes accessed | tf_op | source)
XLA Modules:
  0.0 574.5 jit_solution(16463644382754722437)
XLA Ops:
  0.6 0.7 convert_bitcast_fusion
  1.4 1.7 select_reduce_fusion.gt_ref
  3.1 551.4 %moe.1 = (f32[1024,1024]{1,0:T(8,128)}, f32[1024,1024]{1,0:T(8,128)}, f32[2,1024,512]{2,1,0:T(8,128)}, f32[2,1024,512]{2,1,0:T(8,128)}, f32[2,512,1024]{2,1,0:T(...) custom-call(bf16[1024,1024]{1,0:T(8,128)(2,1)} %x_ref.3, ...), custom_call_target="tpu_custom_call" | custom-call | tf_op jit(solution)/shard_map/moe/pallas_call | solution.py:414
  554.5 19.9 %finish.1 = (bf16[1024,1024]{1,0:T(8,128)(2,1)}, bf16[1024,1024]{1,0:T(8,128)(2,1)}, f32[2,1024,512]{2,1,0:T(8,128)}, f32[2,1024,512]{2,1,0:T(8,128)}, f32[2,512,1024]{2,1,0:T(8,128)}) custom-call(bf16[1024,1024]{1,0:T(8,128)(2,1)} %x_ref.3, bf16[1024,1024]{1,0:T(8,128)(2,1)} %dy_ref.3, bf16[32,1024]{1,0:T(8,128)(2,1)} %select_reduce_fusion.gt_ref, ...), custom_call_target="tpu_custom_call" | custom-call | tf_op jit(solution)/shard_map/finish/pallas_call | solution.py:436
